TPU v7x, 128 devices: a whole 4x4x4 slice. The times are simulated.
128 devices in a mesh: pair: 8 (over x, core), aux: 16 (over y, z).
Axes of the slice: x: 4, y: 4, z: 4, core: 2. Of those that a mesh axis runs over, the one named last changes fastest.
Arguments:
- left_active: bfloat16 [80, 128, 61440], P('pair', None, 'aux'), may hold values from -0.375 to 0.375
- right_active: bfloat16 [80, 128, 61440], P('pair', None, 'aux'), may hold values from -0.375 to 0.375
- amps_active: bfloat16 [80, 128, 128], P('pair', 'aux'), may hold values from -0.5 to 0.5
- rank_active: int32 [80], P('pair'), may hold values from 80 to 128, as said below
- gap_active: float32 [80], P('pair'), may hold values from 0.5 to 2
- energy_active: float32 [80, 128], P('pair'), may hold values from 0.5 to 4
- intersect_active: bfloat16 [80, 4, 128, 128], P('pair'), may hold values from -0.75 to 0.75
- fock_active: float32 [80, 4], P('pair'), may hold values from -2 to 2
- neighbor_active: int32 [80, 4], P('pair'), may hold values from 0 to 79
- left_env: bfloat16 [32, 48, 61440], P('pair', None, 'aux'), may hold values from -0.375 to 0.375
- right_env: bfloat16 [32, 48, 61440], P('pair', None, 'aux'), may hold values from -0.375 to 0.375
- amps_env: bfloat16 [32, 48, 48], P('pair', 'aux'), may hold values from -0.875 to 0.875
- rank_env: int32 [32], P('pair'), may hold values from 24 to 48, as said below
- gap_env: float32 [32], P('pair'), may hold values from 0.5 to 2
- energy_env: float32 [32, 48], P('pair'), may hold values from 0.5 to 4
- intersect_env: bfloat16 [32, 4, 48, 48], P('pair'), may hold values from -1.25 to 1.25
- fock_env: float32 [32, 4], P('pair'), may hold values from -2 to 2
- neighbor_env: int32 [32, 4], P('pair'), may hold values from 0 to 31
Outputs:
- new_active: float32 [80, 128, 128], P('pair', 'aux')
- new_env: float32 [32, 48, 48], P('pair', 'aux')
Inputs may be any that keep to these rules, and one draw needn't show every extreme that they name: `rank_active`: multiples of 8; the first active pair has rank 128. `rank_env`: multiples of 8; the first environment pair has rank 48.
All inputs are finite; a program needn't handle non-finite values.
Results may differ from a plain program's by a relative error of at most 0.0041.
Values may be sent and summed in bfloat16 or wider, within the bound.
No kernel may reach another device: no remote copies, remote signals or barrier semaphores. Data moves between devices by JAX's collectives and lax.ppermute only.
A program may use at most 128 MiB of HBM per device.

v0:
```python
import jax
import jax.numpy as jnp
from jax import lax
from jax.sharding import Mesh
from jax.sharding import PartitionSpec as P

AUX = ("aux_0", "aux_1")


HIGHEST = lax.Precision.HIGHEST


def whole_of(shard, axes, dim):
    result = shard
    for number in range(len(axes) - 1, -1, -1):
        result = lax.all_gather(result, axes[number], axis=dim, tiled=True)
    return result


def joined_along(tiles, dim):
    tiles = jnp.moveaxis(tiles, 0, dim)
    lengths = tiles.shape
    return tiles.reshape(*lengths[:dim], lengths[dim] * lengths[dim + 1], *lengths[dim + 2 :])


def gather_packed(arrays, axis, dims):
    flat = jnp.concatenate([a.reshape(-1) for a in arrays])
    lines, at, gathered = (lax.all_gather(flat, axis), 0, [])
    for a, dim in zip(arrays, dims):
        tiles = lines[:, at : at + a.size].reshape(-1, *a.shape)
        gathered.append(joined_along(tiles, dim))
        at += a.size
    return tuple(gathered)


def split_up(shard, dim, size):
    lengths = shard.shape
    tiles = shard.reshape(*lengths[:dim], size, lengths[dim] // size, *lengths[dim + 1 :])
    return jnp.moveaxis(tiles, dim, 0)


def sum_at_owner(shard, axis, dim):
    size = lax.axis_size(axis)
    tiles = lax.all_to_all(split_up(shard, dim, size), axis, 0, 0, tiled=True)
    return jnp.sum(tiles.astype(jnp.float32), axis=0)


def shard_mask(pair_ranks, row_count, full_width, row_start):
    row_index = row_start + jnp.arange(row_count, dtype=jnp.int32)
    col_index = jnp.arange(full_width, dtype=jnp.int32)
    return (row_index[None, :, None] < pair_ranks[:, None, None]) & (
        col_index[None, None, :] < pair_ranks[:, None, None]
    )


def aux_terms(left_ints, right_ints, own_full, with_ladder):
    summed_terms = jnp.einsum(
        "paq,pbq->pab", left_ints, right_ints, preferred_element_type=jnp.float32
    )
    if with_ladder:
        cross_left = jnp.einsum(
            "pab,paq->pbq", own_full, left_ints, preferred_element_type=jnp.float32
        ).astype(jnp.bfloat16)
        cross_right = jnp.einsum(
            "pab,pbq->paq", own_full, right_ints, preferred_element_type=jnp.float32
        ).astype(jnp.bfloat16)
        summed_terms = summed_terms + jnp.einsum(
            "pcq,pbq->pcb", cross_left, right_ints, preferred_element_type=jnp.float32
        )
        summed_terms = summed_terms + jnp.einsum(
            "pcq,paq->pca", cross_left, cross_right, preferred_element_type=jnp.float32
        )
    return summed_terms


def couple_blocks(cols_over, near_block, intersect, fock_weights):
    right_part = jnp.einsum(
        "pkst,pkut->pksu", near_block, intersect, preferred_element_type=jnp.float32
    )
    right_part = right_part * fock_weights[:, :, None, None]
    return jnp.einsum(
        "pkrs,pksu->pru", cols_over.astype(jnp.float32), right_part, precision=HIGHEST
    )


def finish(summed, amp_shard, pair_ranks, pair_gaps, energy, row_start):
    row_count = amp_shard.shape[1]
    inside = shard_mask(pair_ranks, row_count, amp_shard.shape[2], row_start)
    energy_rows = lax.dynamic_slice_in_dim(energy, row_start, row_count, 1)
    denominator = energy_rows[:, :, None] + energy[:, None, :] + pair_gaps[:, None, None]
    return jnp.where(inside, amp_shard.astype(jnp.float32) - summed / denominator, jnp.float32(0.0))


def shards(
    left_active,
    right_active,
    amps_active,
    rank_active,
    gap_active,
    energy_active,
    intersect_active,
    fock_active,
    neighbor_active,
    left_env,
    right_env,
    amps_env,
    rank_env,
    gap_env,
    energy_env,
    intersect_env,
    fock_env,
    neighbor_env,
):
    aux_place = lax.axis_index(AUX)
    rows_act = amps_active.shape[1]
    rows_env = amps_env.shape[1]
    start_act = aux_place * rows_act
    start_env = aux_place * rows_env
    shard_act = jnp.where(
        shard_mask(rank_active, rows_act, amps_active.shape[2], start_act),
        amps_active,
        jnp.zeros_like(amps_active),
    )
    shard_env = jnp.where(
        shard_mask(rank_env, rows_env, amps_env.shape[2], start_env),
        amps_env,
        jnp.zeros_like(amps_env),
    )
    own_act = whole_of(shard_act, AUX, 1)
    block_act, block_env = gather_packed((shard_act, shard_env), "pair", (0, 0))
    cols_over_act = lax.dynamic_slice_in_dim(intersect_active, start_act, rows_act, 3)
    cols_over_env = lax.dynamic_slice_in_dim(intersect_env, start_env, rows_env, 3)
    terms_act = aux_terms(left_active, right_active, own_act, True) + couple_blocks(
        cols_over_act, block_act[neighbor_active], intersect_active, fock_active
    )
    terms_env = aux_terms(left_env, right_env, None, False) + couple_blocks(
        cols_over_env, block_env[neighbor_env], intersect_env, fock_env
    )
    summed_act, summed_env = (
        sum_at_owner(terms_act.astype(jnp.bfloat16), AUX, 1),
        sum_at_owner(terms_env.astype(jnp.bfloat16), AUX, 1),
    )
    new_active = finish(summed_act, shard_act, rank_active, gap_active, energy_active, start_act)
    new_env = finish(summed_env, shard_env, rank_env, gap_env, energy_env, start_env)
    return (new_active, new_env)


def solution(mesh):
    finer = Mesh(mesh.devices.reshape(mesh.shape["pair"], 4, 4), ("pair", "aux_0", "aux_1"))
    return jax.shard_map(
        shards,
        mesh=finer,
        in_specs=(
            P("pair", None, AUX),
            P("pair", None, AUX),
            P("pair", AUX, None),
            P("pair"),
            P("pair"),
            P("pair", None),
            P("pair", None, None, None),
            P("pair", None),
            P("pair", None),
            P("pair", None, AUX),
            P("pair", None, AUX),
            P("pair", AUX, None),
            P("pair"),
            P("pair"),
            P("pair", None),
            P("pair", None, None, None),
            P("pair", None),
            P("pair", None),
        ),
        out_specs=(P("pair", AUX, None), P("pair", AUX, None)),
        check_vma=False,
    )
```

profile of v0, /device:TPU:0, one launch (start us, length us, event | category | flops | bytes accessed | tf_op | source)
XLA Modules:
  0.0 121.1 jit_solution(1759668718932934217)
XLA Ops:
  7.2 0.0 all-reduce.3.cloned.1.call-start
  7.2 0.8 iota_compare_fusion
  8.1 0.7 broadcast_compare_fusion
  8.8 0.7 iota_compare_fusion.1
  9.5 0.7 broadcast_compare_fusion.1
  10.3 0.8 and_select_fusion.3
  11.0 0.1 reshape.139
  11.1 0.8 fusion.42
  11.9 1.2 %dynamic-slice = u32[1]{0:T(128)} dynamic-slice(u32[128]{0:T(128)} %constant.50, u32[]{:T(128)S(6)} %add.122), dynamic_slice_sizes={1} | dynamic-slice | bytes 12
  13.9 0.5 dynamic-update-slice
  14.4 0.7 copy-done.2
  15.0 0.0 all-reduce.3.cloned.1.call-update
  15.1 0.8 and_select_fusion.1
  15.9 12.2 %all_gather.12 = bf16[10,32,128]{2,1,0:T(8,128)(2,1)S(1)} all-gather(bf16[10,8,128]{2,1,0:T(8,128)(2,1)S(1)} %and_select_fusion.1), channel_id=1, replica_groups=mesh['pair'=8,'aux_0'=4,'aux_1'=4] {'aux_1'}, dimensions={1}, use_global_device_ids=true | all-gather | bytes 102400 | tf_op jit(solution)/shard_map/all_gather | solution.py:16
  28.0 13.1 %all_gather.13 = bf16[10,128,128]{2,1,0:T(8,128)(2,1)S(1)} all-gather(bf16[10,32,128]{2,1,0:T(8,128)(2,1)S(1)} %all_gather.12), channel_id=1, replica_groups=mesh['pair'=8,'aux_0'=4,'aux_1'=4] {'aux_0'}, dimensions={1}, use_global_device_ids=true | all-gather | bytes 409600 | tf_op jit(solution)/shard_map/all_gather | solution.py:16
  41.2 10.4 %convolution_convert_fusion = bf16[10,128,3840]{2,1,0:T(8,128)(2,1)} fusion(bf16[10,128,128]{2,1,0:T(8,128)(2,1)S(1)} %all_gather.13, bf16[10,128,3840]{2,1,0:T(8,128)(2,1)} %param.18), kind=kOutput, calls=%fused_computation.4 | convolution fusion | flops 1263206400 | bytes 19988480 | tf_op jit(solution)/shard_map/pab,paq->pbq/dot_general | solution.py:61
  51.5 9.3 %fusion.24 = f32[10,128,128]{2,1,0:T(8,128)S(1)} fusion(bf16[10,128,3840]{2,1,0:T(8,128)(2,1)} %param.18, bf16[10,128,3840]{2,1,0:T(8,128)(2,1)} %param.19), kind=kOutput, calls=%fused_computation.42 | convolution fusion | flops 1258291200 | bytes 20316160 | tf_op jit(solution)/shard_map/paq,pbq->pab/dot_general | solution.py:57
  60.9 10.2 %convolution_add_fusion = f32[10,128,128]{2,1,0:T(8,128)} fusion(f32[10,128,128]{2,1,0:T(8,128)S(1)} %fusion.24, bf16[10,128,3840]{2,1,0:T(8,128)(2,1)} %convolution_convert_fusion, bf16[10,128,3840]{2,1,0:T(8,128)(2,1)} %param.19), kind=kOutput, calls=%fused_computation.11 | convolution fusion | flops 1258455040 | bytes 20971520 | tf_op jit(solution)/shard_map/pcq,pbq->pcb/dot_general | solution.py:67
  71.1 10.4 %fusion.6 = f32[10,128,128]{2,1,0:T(8,128)} fusion(f32[10,128,128]{2,1,0:T(8,128)} %convolution_add_fusion, bf16[10,128,3840]{2,1,0:T(8,128)(2,1)} %convolution_convert_fusion, bf16[10,128,128]{2,1,0:T(8,128)(2,1)S(1)} %all_gather.13, bf16[10,128,3840]{2,1,0:T(8,128)(2,1)} %param.19), kind=kOutput, calls=%fused_computation.8 | convolution fusion | flops 2521661440 | bytes 21299200 | tf_op jit(solution)/shard_map/pcq,paq->pca/dot_general | solution.py:70
  81.5 0.1 copy.34
  81.6 0.1 reshape.144
  81.7 0.1 copy.35
  81.8 0.1 reshape.152
  81.9 0.1 constant_dynamic-slice_fusion.1
  82.1 0.2 copy.44
  82.2 0.1 constant_dynamic-slice_fusion
  82.3 0.1 copy.40
  82.4 0.1 constant_dynamic-slice_fusion.2
  82.5 1.1 reshape.158
  83.6 0.1 reshape_reshape.6
  83.7 0.1 reshape_reshape.7
  83.8 0.6 gather_fusion.1
  84.4 0.2 convolution_multiply_fusion.1
  84.6 0.3 convolution_bitcast_fusion
  84.9 1.9 %fusion.21 = bf16[4,48,48]{2,1,0:T(8,128)(2,1)S(1)} fusion(f32[4,48,48]{2,1,0:T(8,128)S(1)} %convolution_bitcast_fusion, bf16[4,48,3840]{2,1,0:T(8,128)(2,1)S(1)} %copy-done, bf16[4,48,3840]{2,1,0:T(8,128)(2,1)} %param.28), kind=kOutput, calls=%fused_computation.17 | convolution fusion | flops 70797312 | bytes 3004416 | tf_op jit(solution)/shard_map/paq,pbq->pab/dot_general | solution.py:57
  86.8 0.7 reshape.170
  87.6 5.5 %all-to-all-start.1 = ((bf16[16,2,288]{2,1,0:T(2,128)(2,1)}), bf16[16,2,288]{2,1,0:T(2,128)(2,1)S(1)}, u32[]{:S(2)}, u32[]{:S(2)}) async-start(bf16[16,2,288]{2,1,0:T(2,128)(2,1)} %reshape.170), calls=%async_computation.1 | async-start | bytes 49152 | tf_op jit(solution)/shard_map/all_to_all | solution.py:44
  93.1 0.6 gather_fusion
  93.7 0.8 convolution_multiply_fusion
  94.4 2.2 %fusion.18 = bf16[10,16,8,128]{3,2,1,0:T(8,128)(2,1)S(1)} fusion(f32[10,128,128]{2,1,0:T(8,128)} %fusion.6, f32[10,4,8,128]{3,2,1,0:T(8,128)S(1)} %convolution_multiply_fusion, bf16[10,4,128,128]{3,2,1,0:T(8,128)(2,1)S(1)} %copy-done.1, s32[]{:T(128)S(6)} %select_n.31), kind=kOutput, calls=%fused_computation.13 | convolution fusion | flops 63242240 | bytes 2457604 | tf_op jit(solution)/shard_map/pkrs,pksu->pru/dot_general | solution.py:81
  96.7 0.8 copy.48
  97.4 3.2 %all-to-all-done.1 = bf16[16,2,288]{2,1,0:T(2,128)(2,1)S(1)} async-done(((bf16[16,2,288]{2,1,0:T(2,128)(2,1)}), bf16[16,2,288]{2,1,0:T(2,128)(2,1)S(1)}, u32[]{:S(2)}, u32[]{:S(2)}) %all-to-all-start.1) | async-done | bytes 18464 | tf_op jit(solution)/shard_map/all_to_all | solution.py:44
  100.7 4.0 %all-to-all-start = ((bf16[16,10,8,128]{3,2,1,0:T(8,128)(2,1)}), bf16[16,10,8,128]{3,2,1,0:T(8,128)(2,1)S(1)}, u32[]{:S(2)}, u32[]{:S(2)}) async-start(bf16[16,10,8,128]{3,2,1,0:T(8,128)(2,1)} %bitcast.44), calls=%async_computation | async-start | bytes 655360 | tf_op jit(solution)/shard_map/all_to_all | solution.py:44
  104.7 0.1 reshape.171
  104.8 0.7 and_select_fusion.2
  105.5 8.0 %all-to-all-done = bf16[16,10,8,128]{3,2,1,0:T(8,128)(2,1)S(1)} async-done(((bf16[16,10,8,128]{3,2,1,0:T(8,128)(2,1)}), bf16[16,10,8,128]{3,2,1,0:T(8,128)(2,1)S(1)}, u32[]{:S(2)}, u32[]{:S(2)}) %all-to-all-start) | async-done | bytes 327712 | tf_op jit(solution)/shard_map/all_to_all | solution.py:44
  113.5 0.1 convert_reduce_fusion
  113.6 0.7 and_select_fusion
  (41 shorter events, 0.2 us)
Async XLA Ops:
  7.2 77.7 %copy-start = (bf16[4,48,3840]{2,1,0:T(8,128)(2,1)S(1)}, bf16[4,48,3840]{2,1,0:T(8,128)(2,1)}, u32[]{:S(2)}) copy-start(bf16[4,48,3840]{2,1,0:T(8,128)(2,1)} %param.27) | copy-start | bytes 4423684
  7.2 75.3 %all-reduce.3.cloned.1.call-start = ((), (), s32[]{:S(2)}) async-start(), calls=%async_computation.2 | async-start | bytes 348160
  14.4 0.7 copy-start.2
  71.1 10.4 %copy-start.9 = (s32[10,4]{0,1:T(4,128)S(1)}, s32[10,4]{0,1:T(4,128)}, u32[]{:S(2)}) copy-start(s32[10,4]{0,1:T(4,128)} %param.26) | copy-start | bytes 484
  71.1 10.7 %copy-start.8 = (f32[10,4]{0,1:T(4,128)S(1)}, f32[10,4]{0,1:T(4,128)}, u32[]{:S(2)}) copy-start(f32[10,4]{0,1:T(4,128)} %param.25) | copy-start | bytes 484
  71.1 10.8 %copy-start.10 = (s32[4,4]{1,0:T(4,128)S(1)}, s32[4,4]{1,0:T(4,128)}, u32[]{:S(2)}) copy-start(s32[4,4]{1,0:T(4,128)} %param.35) | copy-start | bytes 196
  71.1 10.9 %copy-start.3 = (bf16[4,4,48,48]{3,2,1,0:T(8,128)(2,1)S(1)}, bf16[4,4,48,48]{3,2,1,0:T(8,128)(2,1)}, u32[]{:S(2)}) copy-start(bf16[4,4,48,48]{3,2,1,0:T(8,128)(2,1)} %param.33) | copy-start | bytes 221188
  71.1 11.1 %copy-start.7 = (f32[4,48]{1,0:T(4,128)S(1)}, f32[4,48]{1,0:T(4,128)}, u32[]{:S(2)}) copy-start(f32[4,48]{1,0:T(4,128)} %param.32) | copy-start | bytes 2308
  71.1 11.3 %copy-start.5 = (f32[10,128]{1,0:T(8,128)S(1)}, f32[10,128]{1,0:T(8,128)}, u32[]{:S(2)}) copy-start(f32[10,128]{1,0:T(8,128)} %param.23) | copy-start | bytes 15364
  71.1 13.3 %copy-start.13 = (f32[4,4]{1,0:T(4,128)S(1)}, f32[4,4]{1,0:T(4,128)}, u32[]{:S(2)}) copy-start(f32[4,4]{1,0:T(4,128)} %param.34) | copy-start | bytes 196
  71.1 22.5 %copy-start.1 = (bf16[10,4,128,128]{3,2,1,0:T(8,128)(2,1)S(1)}, bf16[10,4,128,128]{3,2,1,0:T(8,128)(2,1)}, u32[]{:S(2)}) copy-start(bf16[10,4,128,128]{3,2,1,0:T(8,128)(2,1)} %param.24) | copy-start | bytes 3932164
  81.5 23.3 %copy-start.6 = (bf16[4,3,48]{2,0,1:T(4,128)(2,1)S(1)}, bf16[4,3,48]{2,0,1:T(4,128)(2,1)}, u32[]{:S(2)}) copy-start(bf16[4,3,48]{2,0,1:T(4,128)(2,1)} %param.29) | copy-start | bytes 3460
  81.5 23.3 %copy-start.12 = (f32[4]{0:T(128)S(1)}, f32[4]{0:T(128)}, u32[]{:S(2)}) copy-start(f32[4]{0:T(128)} %param.31) | copy-start | bytes 52
  81.5 32.0 %copy-start.4 = (bf16[10,8,128]{2,1,0:T(8,128)(2,1)S(1)}, bf16[10,8,128]{2,1,0:T(8,128)(2,1)}, u32[]{:S(2)}) copy-start(bf16[10,8,128]{2,1,0:T(8,128)(2,1)} %param.20) | copy-start | bytes 61444
  81.5 32.0 %copy-start.11 = (f32[10]{0:T(128)S(1)}, f32[10]{0:T(128)}, u32[]{:S(2)}) copy-start(f32[10]{0:T(128)} %param.22) | copy-start | bytes 124
  87.6 13.1 %all-to-all-start.1 = ((bf16[16,2,288]{2,1,0:T(2,128)(2,1)}), bf16[16,2,288]{2,1,0:T(2,128)(2,1)S(1)}, u32[]{:S(2)}, u32[]{:S(2)}) async-start(bf16[16,2,288]{2,1,0:T(2,128)(2,1)} %reshape.170), calls=%async_computation.1 | async-start | bytes 49152 | tf_op jit(solution)/shard_map/all_to_all | solution.py:44
  100.7 12.8 %all-to-all-start = ((bf16[16,10,8,128]{3,2,1,0:T(8,128)(2,1)}), bf16[16,10,8,128]{3,2,1,0:T(8,128)(2,1)S(1)}, u32[]{:S(2)}, u32[]{:S(2)}) async-start(bf16[16,10,8,128]{3,2,1,0:T(8,128)(2,1)} %bitcast.44), calls=%async_computation | async-start | bytes 655360 | tf_op jit(solution)/shard_map/all_to_all | solution.py:44
Sparse Core Ops, SparseCore 0:
  15.2 62.6 all-reduce.2
where the time goes:
time: 122 us; the launch traced here: 121 us
  matrix products  45.6 us (37%)
  blocking collectives  25.3 us (21%)
  between operations  15 us (12%)
  waiting for transfers between devices  11.2 us (9%)
  starting transfers between devices  9.5 us (8%)
  local copies, waits for them, and re-layouts  7.61 us (6%)
  other arithmetic  6.92 us (6%)
    all_gather x2, blocking collectives, whole_of(): result = lax.all_gather(result, axes[number], axis=dim, tiled=True)  25.3 us
    dot_general x2, matrix products, aux_terms(): jnp.einsum('paq,pbq->pab', left_ints, right_ints, preferred_element_type=...  11.2 us
    all_to_all x2, waiting for transfers between devices, sum_at_owner(): tiles = lax.all_to_all(split_up(shard, dim, size), axis, 0, 0, tiled=True)  11.2 us
    dot_general x1, matrix products, aux_terms(): jnp.einsum('pcq,paq->pca', cross_left, cross_right, preferred_element_typ...  10.4 us
    dot_general x1, matrix products, aux_terms(): jnp.einsum('pab,paq->pbq', own_full, left_ints, preferred_element_type=jn...  10.4 us
    dot_general x1, matrix products, aux_terms(): jnp.einsum('pcq,pbq->pcb', cross_left, right_ints, preferred_element_type...  10.2 us
    all_to_all x2, starting transfers between devices, sum_at_owner(): tiles = lax.all_to_all(split_up(shard, dim, size), axis, 0, 0, tiled=True)  9.46 us
    unnamed x35, local copies, waits for them, and re-layouts  3.61 us
  transfers between devices with their start and end apart: 3, of which 2 were waited for; matrix products, arithmetic and copies ran while one was open for 39% of the time, Pallas kernels for 0%

commit v1 on v0

v1 whole, which is shorter than its diff:
```python
import jax
import jax.numpy as jnp
from jax import lax
from jax.experimental import pallas as pl
from jax.experimental.pallas import tpu as pltpu
from jax.sharding import PartitionSpec as P

BF16 = jnp.bfloat16
F32 = jnp.float32
VMEM = pl.BlockSpec(memory_space=pltpu.VMEM)
SMEM = pl.BlockSpec(memory_space=pltpu.SMEM)
HBM = pl.BlockSpec(memory_space=pl.ANY)


def dot_nt(left, right):
    return lax.dot_general(left, right, (((1,), (1,)), ((), ())), preferred_element_type=F32)


def dot_nn(left, right):
    return lax.dot_general(left, right, (((1,), (0,)), ((), ())), preferred_element_type=F32)


def dot_tn(left, right):
    return lax.dot_general(left, right, (((0,), (0,)), ((), ())), preferred_element_type=F32)


def cost(flops, nbytes):
    return pl.CostEstimate(flops=flops, bytes_accessed=nbytes, transcendentals=0)


def masked_rows(amps, rank, start):
    rows = start + lax.broadcasted_iota(jnp.int32, amps.shape, 0)
    cols = lax.broadcasted_iota(jnp.int32, amps.shape, 1)
    return jnp.where((rows < rank) & (cols < rank), amps, 0.0)


def pack_kernel(act_ref, env_ref, rank_ref, rank_env_ref, aux_ref, pair_ref):
    place = lax.axis_index("aux")
    n_act, rows_act, _ = act_ref.shape
    n_env, rows_env, width_env = env_ref.shape
    for p in range(n_act):
        block = masked_rows(act_ref[p].astype(F32), rank_ref[p], place * rows_act).astype(BF16)
        for dest in range(aux_ref.shape[0]):
            aux_ref[dest, p] = block
        for dest in range(pair_ref.shape[0]):
            pair_ref[dest, p] = block
    pair_ref[:, n_act:] = jnp.zeros((pair_ref.shape[0], n_env, 8, 128), BF16)
    for p in range(n_env):
        block = masked_rows(env_ref[p].astype(F32), rank_env_ref[p], place * rows_env).astype(BF16)
        for dest in range(pair_ref.shape[0]):
            pair_ref[dest, n_act + p, 0:rows_env, 0:width_env] = block


def ladder_kernel(la_ref, ra_ref, le_ref, re_ref, sa_ref, se_ref, la, ra, le, re, sems):
    n_act, n_env = la_ref.shape[0], le_ref.shape[0]
    copies = []
    for p in range(n_act):
        copies.append((
            pltpu.make_async_copy(la_ref.at[p], la.at[p], sems.at[0, p]),
            pltpu.make_async_copy(ra_ref.at[p], ra.at[p], sems.at[1, p]),
        ))
    for p in range(n_env):
        copies.append((
            pltpu.make_async_copy(le_ref.at[p], le.at[p], sems.at[0, n_act + p]),
            pltpu.make_async_copy(re_ref.at[p], re.at[p], sems.at[1, n_act + p]),
        ))
    for first, second in copies:
        first.start()
        second.start()
    for p in range(n_act):
        copies[p][0].wait()
        copies[p][1].wait()
        sa_ref[p] = dot_nt(la[p], ra[p])
    for p in range(n_env):
        copies[n_act + p][0].wait()
        copies[n_act + p][1].wait()
        se_ref[p] = dot_nt(le[p], re[p])


def combine_kernel(
    sa_ref, se_ref, own_ref, near_ref, xa_ref, xe_ref, fa_ref, na_ref, fe_ref, ne_ref, out_ref
):
    place = lax.axis_index("aux")
    n_act, n_env = sa_ref.shape[0], se_ref.shape[0]
    n_aux = own_ref.shape[0]
    width, width_env = sa_ref.shape[1], se_ref.shape[1]
    rows_env = width_env // n_aux
    tile = lax.broadcasted_iota(jnp.int32, (n_aux, 8, width), 0)
    for p in range(n_act):
        amps = own_ref[:, p].reshape(width, width)
        base = sa_ref[p]
        once = dot_tn(amps, base.astype(BF16))
        twice = dot_nt(once.astype(BF16), amps)
        halves = []
        for k in range(4):
            n = na_ref[p, k]
            near = near_ref[n // n_act, n % n_act]
            half = dot_nt(near, xa_ref[p, k]) * fa_ref[p, k]
            half = jnp.where(tile == place, half[None], 0.0).reshape(width, width)
            halves.append(half.astype(BF16))
        coupled = dot_nn(
            jnp.concatenate([xa_ref[p, k] for k in range(4)], axis=1),
            jnp.concatenate(halves, axis=0),
        )
        total = base + once + twice + coupled
        out_ref[:, p] = total.astype(BF16).reshape(n_aux, 8, width)
    row = lax.broadcasted_iota(jnp.int32, (width_env, 8), 0)
    col = lax.broadcasted_iota(jnp.int32, (width_env, 8), 1)
    pick = jnp.where((row == place * rows_env + col) & (col < rows_env), 1.0, 0.0).astype(BF16)
    env = []
    for p in range(n_env):
        total = se_ref[p]
        for k in range(4):
            n = ne_ref[p, k]
            near = near_ref[n // n_env, n_act + n % n_env][:, 0:width_env]
            half = dot_nt(near, xe_ref[p, k]) * fe_ref[p, k]
            cols = dot_nn(xe_ref[p, k], pick)
            total = total + dot_nn(cols.astype(BF16), half.astype(BF16))
        env.append(total.astype(BF16))
    row = lax.broadcasted_iota(jnp.int32, (n_aux * 8, 2 * width_env), 0)
    col = lax.broadcasted_iota(jnp.int32, (n_aux * 8, 2 * width_env), 1)
    slot = row % 8
    source = jnp.where(slot < rows_env, slot, width_env + slot - rows_env) + rows_env * (row // 8)
    spread = jnp.where((col == source) & (slot < 2 * rows_env), 1.0, 0.0).astype(BF16)
    out_ref[:, n_act] = jnp.zeros((n_aux, 8, width), BF16)
    for side in range(2):
        both = jnp.concatenate([env[2 * side], env[2 * side + 1]], axis=0)
        laid = dot_nn(spread, both).astype(BF16).reshape(n_aux, 8, width_env)
        out_ref[:, n_act, :, 64 * side : 64 * side + width_env] = laid


def own_energies(energy, shape, start):
    row = lax.broadcasted_iota(jnp.int32, shape, 0)
    col = lax.broadcasted_iota(jnp.int32, shape, 1)
    return jnp.sum(jnp.where(col == start + row, energy, 0.0), axis=1, keepdims=True)


def updated(amps, summed, energy, rank, gap, start):
    denominator = own_energies(energy, amps.shape, start) + energy + gap
    rows = start + lax.broadcasted_iota(jnp.int32, amps.shape, 0)
    cols = lax.broadcasted_iota(jnp.int32, amps.shape, 1)
    return jnp.where((rows < rank) & (cols < rank), amps - summed / denominator, 0.0)


def finish_kernel(
    sum_ref, aa_ref, ra_ref, ga_ref, ea_ref, ae_ref, re_ref, ge_ref, ee_ref, oa_ref, oe_ref
):
    place = lax.axis_index("aux")
    n_act, rows_act, _ = aa_ref.shape
    n_env, rows_env, width_env = ae_ref.shape
    for p in range(n_act):
        summed = jnp.sum(sum_ref[:, p].astype(F32), axis=0)
        oa_ref[p] = updated(
            aa_ref[p].astype(F32), summed, ea_ref[p : p + 1], ra_ref[p], ga_ref[p], place * rows_act
        )
    summed = jnp.sum(sum_ref[:, n_act].astype(F32), axis=0)
    for p in range(n_env):
        side, at = p // 2, rows_env * (p % 2)
        mine = summed[at : at + rows_env, 64 * side : 64 * side + width_env]
        oe_ref[p] = updated(
            ae_ref[p].astype(F32), mine, ee_ref[p : p + 1], re_ref[p], ge_ref[p], place * rows_env
        )


def shards(
    left_active, right_active, amps_active, rank_active, gap_active, energy_active,
    intersect_active, fock_active, neighbor_active,
    left_env, right_env, amps_env, rank_env, gap_env, energy_env,
    intersect_env, fock_env, neighbor_env,
):
    n_act, rows_act, width = amps_active.shape
    n_env, rows_env, width_env = amps_env.shape
    n_aux, n_pair = lax.axis_size("aux"), lax.axis_size("pair")
    shape = jax.ShapeDtypeStruct
    for_aux, for_pair = pl.pallas_call(
        pack_kernel,
        out_shape=(
            shape((n_aux, n_act, 8, 128), BF16),
            shape((n_pair, n_act + n_env, 8, 128), BF16),
        ),
        in_specs=[VMEM, VMEM, SMEM, SMEM],
        out_specs=(VMEM, VMEM),
        cost_estimate=cost(10**6, 10**6),
        name="pack",
    )(amps_active, amps_env, rank_active, rank_env)
    own = lax.all_to_all(for_aux, "aux", 0, 0, tiled=True)
    near = lax.all_to_all(for_pair, "pair", 0, 0, tiled=True)
    length = left_active.shape[2]
    sum_act, sum_env = pl.pallas_call(
        ladder_kernel,
        out_shape=(
            shape((n_act, width, width), F32),
            shape((n_env, width_env, width_env), F32),
        ),
        in_specs=[HBM] * 4,
        out_specs=(VMEM, VMEM),
        scratch_shapes=[
            pltpu.VMEM((n_act, width, length), BF16),
            pltpu.VMEM((n_act, width, length), BF16),
            pltpu.VMEM((n_env, width_env, length), BF16),
            pltpu.VMEM((n_env, width_env, length), BF16),
            pltpu.SemaphoreType.DMA((2, n_act + n_env)),
        ],
        compiler_params=pltpu.CompilerParams(vmem_limit_bytes=36 * 1024 * 1024),
        cost_estimate=cost(3 * 10**9, 23 * 10**6),
        name="ladder",
    )(left_active, right_active, left_env, right_env)
    shares = pl.pallas_call(
        combine_kernel,
        out_shape=shape((n_aux, n_act + 1, 8, 128), BF16),
        in_specs=[VMEM] * 6 + [SMEM] * 4,
        out_specs=VMEM,
        cost_estimate=cost(10**9, 3 * 10**6),
        name="combine",
    )(
        sum_act, sum_env, own, near, intersect_active, intersect_env,
        fock_active, neighbor_active, fock_env, neighbor_env,
    )
    summed = lax.all_to_all(shares, "aux", 0, 0, tiled=True)
    return pl.pallas_call(
        finish_kernel,
        out_shape=(
            shape((n_act, rows_act, width), F32),
            shape((n_env, rows_env, width_env), F32),
        ),
        in_specs=[VMEM, VMEM, SMEM, SMEM, VMEM, VMEM, SMEM, SMEM, VMEM],
        out_specs=(VMEM, VMEM),
        cost_estimate=cost(10**6, 10**6),
        name="finish",
    )(
        summed, amps_active, rank_active, gap_active, energy_active,
        amps_env, rank_env, gap_env, energy_env,
    )


def solution(mesh):
    rows = P("pair", "aux", None)
    deep = P("pair", None, "aux")
    per_pair = P("pair")
    level = (
        deep, deep, rows, per_pair, per_pair, P("pair", None),
        P("pair", None, None, None), P("pair", None), P("pair", None),
    )
    return jax.shard_map(
        shards, mesh=mesh, in_specs=level + level, out_specs=(rows, rows), check_vma=False
    )
```

time: 122 us -> 74.7 us (0.61)
  matrix products: 45.6 us -> 0 us
  Pallas kernels: 0 us -> 23.2 us
  between operations: 15 us -> 0.66 us
  waiting for transfers between devices: 11.2 us -> 0.01 us
  other arithmetic: 6.92 us -> 0 us
  local copies, waits for them, and re-layouts: 7.61 us -> 14.1 us
  blocking collectives: 25.3 us -> 28 us
  starting transfers between devices: 9.5 us -> 8.05 us
    dot_general x9 -> x0, matrix products: 45.6 us -> none  [the longest x2 11.2 us: aux_terms(): jnp.einsum('paq,pbq->pab', left_ints, right_ints, preferred_element_type=...]
    all_to_all x0 -> x2, blocking collectives: none -> 28 us  [the longest x1 16.3 us: shards(): summed = lax.all_to_all(shares, 'aux', 0, 0, tiled=True)]
    all_gather x2 -> x0, blocking collectives: 25.3 us -> none  [whole_of(): result = lax.all_gather(result, axes[number], axis=dim, tiled=True)]
    pallas_call x0 -> x4, Pallas kernels: none -> 23.2 us  [the longest x1 12.4 us: shards(): pl.pallas_call(ladder_kernel, out_shape=(shape((n_act, width, width), F32...]
    all_to_all x2 -> x1, waiting for transfers between devices: 11.2 us -> 0.01 us  [shards(): own = lax.all_to_all(for_aux, 'aux', 0, 0, tiled=True)]
    unnamed x35 -> x15, local copies, waits for them, and re-layouts: 3.61 us -> 12.8 us
    lt x4 -> x0, other arithmetic: 3.01 us -> none  [the longest x2 1.56 us: shard_mask(): col_index[None, None, :] < pair_ranks[:, None, None]]
    select_n x6 -> x0, other arithmetic: 2.97 us -> none  [the longest x2 1.4 us: finish(): jnp.where(inside, amp_shard.astype(jnp.float32) - summed / denominator, j...]
  transfers between devices with their start and end apart: 3 -> 1, of which waited for: 2 -> 0; matrix products, arithmetic and copies ran while one was open for 39% -> 4% of each run, Pallas kernels for 0% -> 17%
where the time goes in v1:
time: 74.7 us; the launch traced here: 73.9 us
  blocking collectives  28 us (37%)
  Pallas kernels  23.2 us (31%)
  local copies, waits for them, and re-layouts  14.1 us (19%)
  starting transfers between devices  8.05 us (11%)
    all_to_all x1, blocking collectives, shards(): summed = lax.all_to_all(shares, 'aux', 0, 0, tiled=True)  16.3 us
    unnamed x15, local copies, waits for them, and re-layouts  12.8 us
    pallas_call x1, Pallas kernels, shards(): pl.pallas_call(ladder_kernel, out_shape=(shape((n_act, width, width), F32...  12.4 us
    all_to_all x1, blocking collectives, shards(): near = lax.all_to_all(for_pair, 'pair', 0, 0, tiled=True)  11.7 us
    all_to_all x1, starting transfers between devices, shards(): own = lax.all_to_all(for_aux, 'aux', 0, 0, tiled=True)  8.05 us
    pallas_call x1, Pallas kernels, shards(): pl.pallas_call(combine_kernel, out_shape=shape((n_aux, n_act + 1, 8, 128)...  7.25 us
    pallas_call x1, Pallas kernels, shards(): pl.pallas_call(finish_kernel, out_shape=(shape((n_act, rows_act, width),...  1.87 us
    pallas_call x1, Pallas kernels, shards(): pl.pallas_call(pack_kernel, out_shape=(shape((n_aux, n_act, 8, 128), BF16...  1.69 us
  transfers between devices with their start and end apart: 1, of which 0 were waited for; matrix products, arithmetic and copies ran while one was open for 4% of the time, Pallas kernels for 17%

profile of v1, /device:TPU:0, one launch (start us, length us, event | category | flops | bytes accessed | tf_op | source)
XLA Modules:
  0.0 73.9 jit_solution(16183839751107834731)
XLA Ops:
  0.6 1.3 %copy.20.env_ref.ae_ref = bf16[4,3,48]{2,1,0:T(4,128)(2,1)} copy(bf16[4,3,48]{2,0,1:T(4,128)(2,1)} %param.29) | data formatting | bytes 2304 | tf_op args[11]
  1.9 1.7 %pack.1 = (bf16[16,10,8,128]{3,2,1,0:T(8,128)(2,1)}, bf16[8,14,8,128]{3,2,1,0:T(8,128)(2,1)}) custom-call(bf16[10,8,128]{2,1,0:T(8,128)(2,1)} %aa_ref.1, bf16[4,3,48]{2,1,0:T(4,128)(2,1)} %copy.20.env_ref.ae_ref, s32[10]{0:T(128)} %ra_ref.3, s32[4]{0:T(128)} %re_ref.3), custom_call_target="tpu_custom_call" | custom-call | flops 1000000 | bytes 1000000 | tf_op jit(solution)/shard_map/pack/pallas_call | solution.py:175
  3.6 11.7 %all_to_all.15.near_ref = bf16[8,14,8,128]{3,2,1,0:T(8,128)(2,1)} all-to-all(bf16[8,14,8,128]{3,2,1,0:T(8,128)(2,1)} %get-tuple-element.9), channel_id=1, replica_groups=mesh['pair'=8,'aux'=16] {'pair'}, dimensions={0} | all-to-all | bytes 458752 | tf_op jit(solution)/shard_map/all_to_all | solution.py:187
  15.3 8.0 %all-to-all-start = ((bf16[16,10,8,128]{3,2,1,0:T(8,128)(2,1)}), bf16[16,10,8,128]{3,2,1,0:T(8,128)(2,1)S(1)}, u32[]{:S(2)}, u32[]{:S(2)}) async-start(bf16[16,10,8,128]{3,2,1,0:T(8,128)(2,1)} %get-tuple-element.8), calls=%async_computation | async-start | bytes 655360 | tf_op jit(solution)/shard_map/all_to_all | solution.py:186
  23.3 1.4 %copy.21.fa_ref = f32[10,4]{1,0:T(8,128)} copy(f32[10,4]{0,1:T(4,128)} %param.25) | data formatting | bytes 320 | tf_op args[7]
  24.7 1.4 %copy.22.na_ref = s32[10,4]{1,0:T(8,128)} copy(s32[10,4]{0,1:T(4,128)} %param.26) | data formatting | bytes 320 | tf_op args[8]
  26.1 0.0 copy-start
  26.1 3.8 %copy-done = bf16[10,128,3840]{2,1,0:T(8,128)(2,1)S(1)} copy-done((bf16[10,128,3840]{2,1,0:T(8,128)(2,1)S(1)}, bf16[10,128,3840]{2,1,0:T(8,128)(2,1)}, u32[]{:S(2)}) %copy-start) | copy-done | bytes 9830424
  29.8 0.0 copy-start.1
  29.8 1.4 %copy-done.1 = bf16[4,48,3840]{2,1,0:T(8,128)(2,1)S(1)} copy-done((bf16[4,48,3840]{2,1,0:T(8,128)(2,1)S(1)}, bf16[4,48,3840]{2,1,0:T(8,128)(2,1)}, u32[]{:S(2)}) %copy-start.1) | copy-done | bytes 1474584
  31.2 0.0 copy-start.2
  31.2 1.4 %copy-done.2 = bf16[4,48,3840]{2,1,0:T(8,128)(2,1)S(1)} copy-done((bf16[4,48,3840]{2,1,0:T(8,128)(2,1)S(1)}, bf16[4,48,3840]{2,1,0:T(8,128)(2,1)}, u32[]{:S(2)}) %copy-start.2) | copy-done | bytes 1474584
  32.6 12.4 %ladder.1 = (f32[10,128,128]{2,1,0:T(8,128)S(1)}, f32[4,48,48]{2,1,0:T(8,128)S(1)}) custom-call(bf16[10,128,3840]{2,1,0:T(8,128)(2,1)S(1)} %copy-done, bf16[10,128,3840]{2,1,0:T(8,128)(2,1)} %ra_ref.2, bf16[4,48,3840]{2,1,0:T(8,128)(2,1)S(1)} %copy-done.1, bf16[4,48,3840]{2,1,0:T(8,128)(2,1)S(1)} %copy-done.2), custom_call_target="tpu_custom_call" | custom-call | flops 3000000000 | bytes 23000000 | tf_op jit(solution)/shard_map/ladder/pallas_call | solution.py:189
  45.0 0.0 copy-start.3
  45.0 0.8 %copy-done.3 = f32[10,128,128]{2,1,0:T(8,128)} copy-done((f32[10,128,128]{2,1,0:T(8,128)}, f32[10,128,128]{2,1,0:T(8,128)S(1)}, u32[]{:S(2)}) %copy-start.3) | copy-done | bytes 655384
  45.8 0.0 copy-start.4
  45.8 0.6 copy-done.4
  46.5 0.0 all-to-all-done.own_ref
  46.5 0.0 copy-start.5
  46.5 0.7 %copy-done.5 = bf16[16,10,8,128]{3,2,1,0:T(8,128)(2,1)} copy-done((bf16[16,10,8,128]{3,2,1,0:T(8,128)(2,1)}, bf16[16,10,8,128]{3,2,1,0:T(8,128)(2,1)S(1)}, u32[]{:S(2)}) %copy-start.5) | copy-done | bytes 327704
  47.2 7.2 %combine.1 = bf16[16,11,8,128]{3,2,1,0:T(8,128)(2,1)} custom-call(f32[10,128,128]{2,1,0:T(8,128)} %copy-done.3, f32[4,48,48]{2,1,0:T(8,128)} %copy-done.4, bf16[16,10,8,128]{3,2,1,0:T(8,128)(2,1)} %copy-done.5, bf16[8,14,8,128]{3,2,1,0:T(8,128)(2,1)} %all_to_all.15.near_ref, bf16[10,4,128,128]{3,2,1,0:T(8,128)(2,1)} %xa_ref.1, ...), custom_call_target="tpu_custom_call" | custom-call | flops 1000000000 | bytes 3000000 | tf_op jit(solution)/shard_map/combine/pallas_call | solution.py:208
  54.5 16.3 %all_to_all.16.sum_ref = bf16[16,11,8,128]{3,2,1,0:T(8,128)(2,1)} all-to-all(bf16[16,11,8,128]{3,2,1,0:T(8,128)(2,1)} %combine.1), channel_id=1, replica_groups=mesh['pair'=8,'aux'=16] {'aux'}, dimensions={0} | all-to-all | bytes 720896 | tf_op jit(solution)/shard_map/all_to_all | solution.py:219
  70.8 1.9 %finish.1 = (f32[10,8,128]{2,1,0:T(8,128)}, f32[4,3,48]{2,1,0:T(4,128)}) custom-call(bf16[16,11,8,128]{3,2,1,0:T(8,128)(2,1)} %all_to_all.16.sum_ref, bf16[10,8,128]{2,1,0:T(8,128)(2,1)} %aa_ref.1, s32[10]{0:T(128)} %ra_ref.3, f32[10]{0:T(128)} %ga_ref.1, f32[10,128]{1,0:T(8,128)} %ea_ref.1, bf16[4,3,48]{2,1,0:T(4,128)(2,1)} %copy.20.env_ref.ae_ref, ...), custom_call_target="tpu_custom_call" | custom-call | flops 1000000 | bytes 1000000 | tf_op jit(solution)/shard_map/finish/pallas_call | solution.py:220
  72.6 1.3 %copy.24 = f32[4,3,48]{2,0,1:T(4,128)} copy(f32[4,3,48]{2,1,0:T(4,128)} %get-tuple-element.11) | data formatting | bytes 4608 | tf_op jit(solution)/shard_map/finish/pallas_call | solution.py:220
Async XLA Ops:
  15.3 31.2 %all-to-all-start = ((bf16[16,10,8,128]{3,2,1,0:T(8,128)(2,1)}), bf16[16,10,8,128]{3,2,1,0:T(8,128)(2,1)S(1)}, u32[]{:S(2)}, u32[]{:S(2)}) async-start(bf16[16,10,8,128]{3,2,1,0:T(8,128)(2,1)} %get-tuple-element.8), calls=%async_computation | async-start | bytes 655360 | tf_op jit(solution)/shard_map/all_to_all | solution.py:186
  26.1 3.8 %copy-start = (bf16[10,128,3840]{2,1,0:T(8,128)(2,1)S(1)}, bf16[10,128,3840]{2,1,0:T(8,128)(2,1)}, u32[]{:S(2)}) copy-start(bf16[10,128,3840]{2,1,0:T(8,128)(2,1)} %la_ref.1) | copy-start | bytes 29491204
  29.8 1.4 %copy-start.1 = (bf16[4,48,3840]{2,1,0:T(8,128)(2,1)S(1)}, bf16[4,48,3840]{2,1,0:T(8,128)(2,1)}, u32[]{:S(2)}) copy-start(bf16[4,48,3840]{2,1,0:T(8,128)(2,1)} %le_ref.1) | copy-start | bytes 4423684
  31.2 1.4 %copy-start.2 = (bf16[4,48,3840]{2,1,0:T(8,128)(2,1)S(1)}, bf16[4,48,3840]{2,1,0:T(8,128)(2,1)}, u32[]{:S(2)}) copy-start(bf16[4,48,3840]{2,1,0:T(8,128)(2,1)} %re_ref.2) | copy-start | bytes 4423684
  45.0 0.8 %copy-start.3 = (f32[10,128,128]{2,1,0:T(8,128)}, f32[10,128,128]{2,1,0:T(8,128)S(1)}, u32[]{:S(2)}) copy-start(f32[10,128,128]{2,1,0:T(8,128)S(1)} %get-tuple-element.6.sa_ref) | copy-start | bytes 1966084
  45.8 0.7 copy-start.4
  46.5 0.8 %copy-start.5 = (bf16[16,10,8,128]{3,2,1,0:T(8,128)(2,1)}, bf16[16,10,8,128]{3,2,1,0:T(8,128)(2,1)S(1)}, u32[]{:S(2)}) copy-start(bf16[16,10,8,128]{3,2,1,0:T(8,128)(2,1)S(1)} %all-to-all-done.own_ref) | copy-start | bytes 983044

commit v2 on v1

v2 whole, which is shorter than its diff:
```python
import jax
import jax.numpy as jnp
from jax import lax
from jax.experimental import pallas as pl
from jax.experimental.pallas import tpu as pltpu
from jax.sharding import PartitionSpec as P


BF16 = jnp.bfloat16
F32 = jnp.float32
VMEM = pl.BlockSpec(memory_space=pltpu.VMEM)
SMEM = pl.BlockSpec(memory_space=pltpu.SMEM)
HBM = pl.BlockSpec(memory_space=pl.ANY)
BIG = pltpu.CompilerParams(vmem_limit_bytes=60 * 1024 * 1024)
SMALL = pltpu.CompilerParams(vmem_limit_bytes=8 * 1024 * 1024)


def dot_nt(left, right):
    return lax.dot_general(left, right, (((1,), (1,)), ((), ())), preferred_element_type=F32)


def dot_nn(left, right):
    return lax.dot_general(left, right, (((1,), (0,)), ((), ())), preferred_element_type=F32)


def dot_tn(left, right):
    return lax.dot_general(left, right, (((0,), (0,)), ((), ())), preferred_element_type=F32)


def cost(flops, nbytes):
    return pl.CostEstimate(flops=flops, bytes_accessed=nbytes, transcendentals=0)


def masked_rows(amps, rank, start):
    rows = start + lax.broadcasted_iota(jnp.int32, amps.shape, 0)
    cols = lax.broadcasted_iota(jnp.int32, amps.shape, 1)
    return jnp.where((rows < rank) & (cols < rank), amps, 0.0)


def pack_kernel(act_ref, env_ref, rank_ref, rank_env_ref, aux_ref, block_ref):
    place = lax.axis_index("aux")
    n_act, rows_act, _ = act_ref.shape
    rows_env, n_env, width_env = env_ref.shape
    for p in range(n_act):
        block = masked_rows(act_ref[p].astype(F32), rank_ref[p], place * rows_act).astype(BF16)
        for dest in range(aux_ref.shape[0]):
            aux_ref[dest, p] = block
        block_ref[p] = block
    block_ref[n_act:] = jnp.zeros((n_env, 8, 128), BF16)
    for p in range(n_env):
        block = masked_rows(env_ref[:, p].astype(F32), rank_env_ref[p], place * rows_env).astype(BF16)
        block_ref[n_act + p, 0:rows_env, 0:width_env] = block


def mark_kernel(block_ref, mark_ref):
    mark_ref[...] = jnp.zeros(mark_ref.shape, F32)


def ladder_kernel(la_ref, ra_ref, le_ref, re_ref, own_ref, mark_ref, sa_ref, se_ref):
    width = sa_ref.shape[1]
    for p in range(la_ref.shape[0]):
        sa_ref[p] = dot_nt(la_ref[p], ra_ref[p])
    for p in range(la_ref.shape[0]):
        amps = own_ref[:, p].reshape(width, width)
        base = sa_ref[p]
        once = dot_tn(amps, base.astype(BF16))
        twice = dot_nt(once.astype(BF16), amps)
        sa_ref[p] = base + once + twice
    for p in range(le_ref.shape[0]):
        se_ref[p] = dot_nt(le_ref[p], re_ref[p])


def combine_kernel(sa_ref, se_ref, *refs):
    n_near = len(refs) - 8
    near_refs = refs[:n_near]
    xa_ref, xe_ref, fa_ref, na_ref, fe_ref, ne_ref, out_ref, near_ref = refs[n_near:]
    place, group = lax.axis_index("aux"), lax.axis_index("pair")
    n_aux, (n_act, width, _) = out_ref.shape[0], sa_ref.shape
    n_env, width_env, _ = se_ref.shape
    rows_env = width_env // n_aux
    tile = lax.broadcasted_iota(jnp.int32, (n_aux, 8, width), 0)
    chips = n_near // 2
    for slot in range(n_near):
        near_ref[slot] = near_refs[slot][...]

    def near_block(n, count, first):
        source = n // count
        slot = (group // 2 + chips - source // 2) % chips + chips * ((group + source) % 2)
        return near_ref[slot, first + n % count]

    for p in range(n_act):
        halves = []
        for k in range(4):
            half = dot_nt(near_block(na_ref[k, p], n_act, 0), xa_ref[p, k]) * fa_ref[k, p]
            half = jnp.where(tile == place, half[None], 0.0).reshape(width, width)
            halves.append(half.astype(BF16))
        coupled = dot_nn(
            jnp.concatenate([xa_ref[p, k] for k in range(4)], axis=1),
            jnp.concatenate(halves, axis=0),
        )
        out_ref[:, p] = (sa_ref[p] + coupled).astype(BF16).reshape(n_aux, 8, width)
    row = lax.broadcasted_iota(jnp.int32, (width_env, 8), 0)
    col = lax.broadcasted_iota(jnp.int32, (width_env, 8), 1)
    pick = jnp.where((row == place * rows_env + col) & (col < rows_env), 1.0, 0.0).astype(BF16)
    env = []
    for p in range(n_env):
        total = se_ref[p]
        for k in range(4):
            near = near_block(ne_ref[p, k], n_env, n_act)[:, 0:width_env]
            half = dot_nt(near, xe_ref[p, k]) * fe_ref[p, k]
            cols = dot_nn(xe_ref[p, k], pick)
            total = total + dot_nn(cols.astype(BF16), half.astype(BF16))
        env.append(total.astype(BF16))
    row = lax.broadcasted_iota(jnp.int32, (n_aux * 8, 2 * width_env), 0)
    col = lax.broadcasted_iota(jnp.int32, (n_aux * 8, 2 * width_env), 1)
    slot = row % 8
    source = jnp.where(slot < rows_env, slot, width_env + slot - rows_env) + rows_env * (row // 8)
    spread = jnp.where((col == source) & (slot < 2 * rows_env), 1.0, 0.0).astype(BF16)
    out_ref[:, n_act] = jnp.zeros((n_aux, 8, width), BF16)
    for side in range(2):
        both = jnp.concatenate([env[2 * side], env[2 * side + 1]], axis=0)
        laid = dot_nn(spread, both).astype(BF16).reshape(n_aux, 8, width_env)
        out_ref[:, n_act, :, 64 * side : 64 * side + width_env] = laid


def own_energies(energy, shape, start):
    row = lax.broadcasted_iota(jnp.int32, shape, 0)
    col = lax.broadcasted_iota(jnp.int32, shape, 1)
    return jnp.sum(jnp.where(col == start + row, energy, 0.0), axis=1, keepdims=True)


def updated(amps, summed, energy, rank, gap, start):
    denominator = own_energies(energy, amps.shape, start) + energy + gap
    rows = start + lax.broadcasted_iota(jnp.int32, amps.shape, 0)
    cols = lax.broadcasted_iota(jnp.int32, amps.shape, 1)
    return jnp.where((rows < rank) & (cols < rank), amps - summed / denominator, 0.0)


def finish_kernel(
    sum_ref, aa_ref, ra_ref, ga_ref, ea_ref, ae_ref, re_ref, ge_ref, ee_ref, oa_ref, oe_ref
):
    place = lax.axis_index("aux")
    n_act, rows_act, _ = aa_ref.shape
    rows_env, n_env, width_env = ae_ref.shape
    for p in range(n_act):
        summed = jnp.sum(sum_ref[:, p].astype(F32), axis=0)
        oa_ref[p] = updated(
            aa_ref[p].astype(F32), summed, ea_ref[p : p + 1], ra_ref[p], ga_ref[p], place * rows_act
        )
    summed = jnp.sum(sum_ref[:, n_act].astype(F32), axis=0)
    for p in range(n_env):
        side, at = p // 2, rows_env * (p % 2)
        mine = summed[at : at + rows_env, 64 * side : 64 * side + width_env]
        oe_ref[:, p] = updated(
            ae_ref[:, p].astype(F32), mine, ee_ref[p : p + 1], re_ref[p], ge_ref[p], place * rows_env
        )


def shards(
    left_active, right_active, amps_active, rank_active, gap_active, energy_active,
    intersect_active, fock_active, neighbor_active,
    left_env, right_env, amps_env, rank_env, gap_env, energy_env,
    intersect_env, fock_env, neighbor_env,
):
    n_act, rows_act, width = amps_active.shape
    n_env, rows_env, width_env = amps_env.shape
    n_aux, n_pair = lax.axis_size("aux"), lax.axis_size("pair")
    shape = jax.ShapeDtypeStruct
    amps_env_t = amps_env.transpose(1, 0, 2)
    for_aux, block = pl.pallas_call(
        pack_kernel,
        out_shape=(
            shape((n_aux, n_act, 8, 128), BF16),
            shape((n_act + n_env, 8, 128), BF16),
        ),
        in_specs=[VMEM, VMEM, SMEM, SMEM],
        out_specs=(VMEM, VMEM),
        compiler_params=BIG,
        cost_estimate=cost(10**6, 10**6),
        name="pack",
    )(amps_active, amps_env_t, rank_active, rank_env)
    ring, near = [block], []
    mark = pl.pallas_call(
        mark_kernel,
        out_shape=shape((8, 128), F32),
        in_specs=[HBM],
        out_specs=VMEM,
        compiler_params=SMALL,
        cost_estimate=cost(3 * 10**10, 10**4),
        name="mark",
    )(block)
    for step in range(1, n_pair // 2):
        route = [(i, (i + 2 * step) % n_pair) for i in range(n_pair)]
        ring.append(lax.ppermute(block, "pair", route))
    own = lax.all_to_all(for_aux, "aux", 0, 0, tiled=True)
    partner = [(i, i ^ 1) for i in range(n_pair)]
    near = ring + [lax.ppermute(x, "pair", partner) for x in ring]
    sum_act, sum_env = pl.pallas_call(
        ladder_kernel,
        out_shape=[shape((n_act, width, width), F32), shape((n_env, width_env, width_env), F32)],
        in_specs=[VMEM] * 5 + [HBM],
        out_specs=[VMEM] * 2,
        compiler_params=SMALL,
        cost_estimate=cost(3 * 10**9, 23 * 10**6),
        name="ladder",
    )(left_active, right_active, left_env, right_env, own, mark)
    shares = pl.pallas_call(
        combine_kernel,
        out_shape=shape((n_aux, n_act + 1, 8, 128), BF16),
        in_specs=[VMEM] * (4 + len(near)) + [SMEM] * 4,
        out_specs=VMEM,
        scratch_shapes=[
            pltpu.VMEM((len(near), n_act + n_env, 8, 128), BF16),
        ],
        compiler_params=SMALL,
        cost_estimate=cost(10**9, 3 * 10**6),
        name="combine",
    )(
        sum_act, sum_env, *near, intersect_active, intersect_env,
        fock_active.T, neighbor_active.T, fock_env, neighbor_env,
    )
    summed = lax.all_to_all(shares, "aux", 0, 0, tiled=True)
    new_active, new_env = pl.pallas_call(
        finish_kernel,
        out_shape=(
            shape((n_act, rows_act, width), F32),
            shape((rows_env, n_env, width_env), F32),
        ),
        in_specs=[VMEM, VMEM, SMEM, SMEM, VMEM, VMEM, SMEM, SMEM, VMEM],
        out_specs=(VMEM, VMEM),
        compiler_params=SMALL,
        cost_estimate=cost(10**6, 10**6),
        name="finish",
    )(
        summed, amps_active, rank_active, gap_active, energy_active,
        amps_env_t, rank_env, gap_env, energy_env,
    )
    return new_active, new_env.transpose(1, 0, 2)


def solution(mesh):
    rows = P("pair", "aux", None)
    deep = P("pair", None, "aux")
    per_pair = P("pair")
    level = (
        deep, deep, rows, per_pair, per_pair, P("pair", None),
        P("pair", None, None, None), P("pair", None), P("pair", None),
    )
    return jax.shard_map(
        shards, mesh=mesh, in_specs=level + level, out_specs=(rows, rows), check_vma=False
    )
```

time: 74.7 us -> 54.5 us (0.73)
  blocking collectives: 28 us -> 12.5 us
  Pallas kernels: 23.2 us -> 11.2 us
  waiting for transfers between devices: 0.01 us -> 7.48 us
  local copies, waits for them, and re-layouts: 14.1 us -> 8.43 us
  starting transfers between devices: 8.05 us -> 13.3 us
    all_to_all x1 -> x0, blocking collectives: 11.7 us -> none  [shards(): near = lax.all_to_all(for_pair, 'pair', 0, 0, tiled=True)]
    pallas_call x1 -> x2, Pallas kernels: 12.4 us -> 3.82 us  [the longest x1 3.82 us: shards(): pl.pallas_call(ladder_kernel, out_shape=[shape((n_act, width, width), F32...]
    all_to_all x1, waiting for transfers between devices: 0.01 us -> 7.46 us  [shards(): own = lax.all_to_all(for_aux, 'aux', 0, 0, tiled=True)]
    ppermute x0 -> x7, starting transfers between devices: none -> 5.24 us  [the longest x3 4.56 us: shards(): ring.append(lax.ppermute(block, 'pair', route))]
    unnamed x15 -> x40, local copies, waits for them, and re-layouts: 12.8 us -> 8.43 us
    all_to_all x1, blocking collectives: 16.3 us -> 12.5 us  [shards(): summed = lax.all_to_all(shares, 'aux', 0, 0, tiled=True)]
    pallas_call x1, Pallas kernels: 7.25 us -> 4.43 us  [shards(): pl.pallas_call(combine_kernel, out_shape=shape((n_aux, n_act + 1, 8, 128)...]
    pallas_call x1 -> x0, local copies, waits for them, and re-layouts: 1.29 us -> none  [shards(): pl.pallas_call(finish_kernel, out_shape=(shape((n_act, rows_act, width),...]
  transfers between devices with their start and end apart: 1 -> 8, of which waited for: 0 -> 1; matrix products, arithmetic and copies ran while one was open for 4% -> 0% of each run, Pallas kernels for 17% -> 7%
where the time goes in v2:
time: 54.5 us; the launch traced here: 53.8 us
  starting transfers between devices  13.3 us (24%)
  blocking collectives  12.5 us (23%)
  Pallas kernels  11.2 us (21%)
  local copies, waits for them, and re-layouts  8.43 us (15%)
  waiting for transfers between devices  7.48 us (14%)
  between operations  0.92 us (2%)
    all_to_all x1, blocking collectives, shards(): summed = lax.all_to_all(shares, 'aux', 0, 0, tiled=True)  12.5 us
    unnamed x40, local copies, waits for them, and re-layouts  8.43 us
    all_to_all x1, starting transfers between devices, shards(): own = lax.all_to_all(for_aux, 'aux', 0, 0, tiled=True)  8.05 us
    all_to_all x1, waiting for transfers between devices, shards(): own = lax.all_to_all(for_aux, 'aux', 0, 0, tiled=True)  7.46 us
    ppermute x3, starting transfers between devices, shards(): ring.append(lax.ppermute(block, 'pair', route))  4.56 us
    pallas_call x1, Pallas kernels, shards(): pl.pallas_call(combine_kernel, out_shape=shape((n_aux, n_act + 1, 8, 128)...  4.43 us
    pallas_call x1, Pallas kernels, shards(): pl.pallas_call(ladder_kernel, out_shape=[shape((n_act, width, width), F32...  3.82 us
    pallas_call x1, Pallas kernels, shards(): pl.pallas_call(pack_kernel, out_shape=(shape((n_aux, n_act, 8, 128), BF16...  1.59 us
  transfers between devices with their start and end apart: 8, of which 1 were waited for; matrix products, arithmetic and copies ran while one was open for 0% of the time, Pallas kernels for 7%

profile of v2, /device:TPU:0, one launch (start us, length us, event | category | flops | bytes accessed | tf_op | source)
XLA Modules:
  0.0 53.8 jit_solution(12969645142476295544)
XLA Ops:
  0.6 1.6 %pack.1 = (bf16[16,10,8,128]{3,2,1,0:T(8,128)(2,1)}, bf16[14,8,128]{2,1,0:T(8,128)(2,1)}) custom-call(bf16[10,8,128]{2,1,0:T(8,128)(2,1)} %aa_ref.1, bf16[3,4,48]{2,1,0:T(4,128)(2,1)} %bitcast.4, s32[10]{0:T(128)} %ra_ref.3, s32[4]{0:T(128)} %re_ref.3), custom_call_target="tpu_custom_call" | custom-call | flops 1000000 | bytes 1000000 | tf_op jit(solution)/shard_map/pack/pallas_call | solution.py:170
  2.2 0.0 collective-permute-start.3
  2.2 2.9 %collective-permute-start.2 = (bf16[14,8,128]{2,1,0:T(8,128)(2,1)}, bf16[14,8,128]{2,1,0:T(8,128)(2,1)}, u32[]{:S(2)}, u32[]{:S(2)}) collective-permute-start(bf16[14,8,128]{2,1,0:T(8,128)(2,1)} %get-tuple-element.9.block_ref.refs_0_), channel_id=1, source_target_pairs={{0,96},{16,112},{32,0},{48,16},{64,32},{80,48},{96,64},{112,80},{1... | collective-permute-start | bytes 86024 | tf_op jit(solution)/shard_map/ppermute | solution.py:194
  5.1 0.8 %collective-permute-start.1 = (bf16[14,8,128]{2,1,0:T(8,128)(2,1)}, bf16[14,8,128]{2,1,0:T(8,128)(2,1)}, u32[]{:S(2)}, u32[]{:S(2)}) collective-permute-start(bf16[14,8,128]{2,1,0:T(8,128)(2,1)} %get-tuple-element.9.block_ref.refs_0_), channel_id=1, source_target_pairs={{0,64},{16,80},{32,96},{48,112},{64,0},{80,16},{96,32},{112,48},{1... | collective-permute-start | bytes 86024 | tf_op jit(solution)/shard_map/ppermute | solution.py:194
  5.9 0.9 %collective-permute-start = (bf16[14,8,128]{2,1,0:T(8,128)(2,1)}, bf16[14,8,128]{2,1,0:T(8,128)(2,1)}, u32[]{:S(2)}, u32[]{:S(2)}) collective-permute-start(bf16[14,8,128]{2,1,0:T(8,128)(2,1)} %get-tuple-element.9.block_ref.refs_0_), channel_id=1, source_target_pairs={{0,32},{16,48},{32,64},{48,80},{64,96},{80,112},{96,0},{112,16},{1... | collective-permute-start | bytes 86024 | tf_op jit(solution)/shard_map/ppermute | solution.py:194
  6.8 8.0 %all-to-all-start = ((bf16[16,10,8,128]{3,2,1,0:T(8,128)(2,1)}), bf16[16,10,8,128]{3,2,1,0:T(8,128)(2,1)S(1)}, u32[]{:S(2)}, u32[]{:S(2)}) async-start(bf16[16,10,8,128]{3,2,1,0:T(8,128)(2,1)} %get-tuple-element.8), calls=%async_computation | async-start | bytes 655360 | tf_op jit(solution)/shard_map/all_to_all | solution.py:195
  14.8 0.0 copy-start.14
  14.9 0.7 %copy-done.14 = bf16[14,8,128]{2,1,0:T(8,128)(2,1)S(1)} copy-done((bf16[14,8,128]{2,1,0:T(8,128)(2,1)S(1)}, bf16[14,8,128]{2,1,0:T(8,128)(2,1)}, u32[]{:S(2)}) %copy-start.14) | copy-done | bytes 28696
  15.6 0.0 copy-start.16
  15.6 0.0 copy-start.17
  15.6 0.0 copy-start.18
  15.6 0.0 copy-start.19
  15.7 0.0 collective-permute-done.2.refs_3_
  15.7 0.1 collective-permute-start.6
  15.8 0.0 collective-permute-done.1.refs_2_
  15.8 0.5 collective-permute-start.5
  16.3 0.0 collective-permute-done.refs_1_
  16.3 0.1 collective-permute-start.4
  16.4 7.5 %all-to-all-done.own_ref = bf16[16,10,8,128]{3,2,1,0:T(8,128)(2,1)S(1)} async-done(((bf16[16,10,8,128]{3,2,1,0:T(8,128)(2,1)}), bf16[16,10,8,128]{3,2,1,0:T(8,128)(2,1)S(1)}, u32[]{:S(2)}, u32[]{:S(2)}) %all-to-all-start) | async-done | bytes 327712 | tf_op jit(solution)/shard_map/all_to_all | solution.py:195
  23.8 0.0 copy-done.2
  23.8 0.0 copy-done.3
  23.8 3.8 %copy-done = bf16[10,128,3840]{2,1,0:T(8,128)(2,1)S(1)} copy-done((bf16[10,128,3840]{2,1,0:T(8,128)(2,1)S(1)}, bf16[10,128,3840]{2,1,0:T(8,128)(2,1)}, u32[]{:S(2)}) %copy-start) | copy-done | bytes 9830424
  27.6 3.8 %copy-done.1 = bf16[10,128,3840]{2,1,0:T(8,128)(2,1)S(1)} copy-done((bf16[10,128,3840]{2,1,0:T(8,128)(2,1)S(1)}, bf16[10,128,3840]{2,1,0:T(8,128)(2,1)}, u32[]{:S(2)}) %copy-start.1) | copy-done | bytes 9830424
  31.4 3.8 %ladder.1 = (f32[10,128,128]{2,1,0:T(8,128)S(1)}, f32[4,48,48]{2,1,0:T(8,128)S(1)}) custom-call(bf16[10,128,3840]{2,1,0:T(8,128)(2,1)S(1)} %copy-done, bf16[10,128,3840]{2,1,0:T(8,128)(2,1)S(1)} %copy-done.1, bf16[4,48,3840]{2,1,0:T(8,128)(2,1)S(1)} %copy-done.2, bf16[4,48,3840]{2,1,0:T(8,128)(2,1)S(1)} %copy-done.3, ...), custom_call_target="tpu_custom_call" | custom-call | flops 3000000000 | bytes 23000000 | tf_op jit(solution)/shard_map/ladder/pallas_call | solution.py:198
  35.3 0.0 collective-permute-done.3.refs_4_
  35.3 0.0 collective-permute-done.6.refs_7_
  35.3 0.0 collective-permute-done.5.refs_6_
  35.3 0.0 collective-permute-done.4.refs_5_
  35.3 0.0 copy-done.13
  35.3 0.0 copy-done.15
  35.3 0.0 copy-done.16
  35.3 0.0 copy-done.17
  35.3 0.0 copy-done.18
  35.3 0.0 copy-done.19
  35.4 0.0 copy-done.12
  35.4 0.0 copy-start.4
  35.4 0.0 copy-start.5
  35.4 0.0 copy-start.6
  35.4 0.0 copy-start.7
  35.4 0.0 copy-start.8
  35.4 0.0 copy-start.9
  35.4 0.0 copy-start.10
  35.4 0.0 copy-start.11
  35.5 4.4 %combine.1 = bf16[16,11,8,128]{3,2,1,0:T(8,128)(2,1)S(1)} custom-call(f32[10,128,128]{2,1,0:T(8,128)S(1)} %get-tuple-element.10.sa_ref, f32[4,48,48]{2,1,0:T(8,128)S(1)} %get-tuple-element.11.se_ref, bf16[14,8,128]{2,1,0:T(8,128)(2,1)S(1)} %copy-done.15, bf16[14,8,128]{2,1,0:T(8,128)(2,1)} %collective-permute-done.refs_1_, ...), custom_call_target="tpu_custom_call" | custom-call | flops 1000000000 | bytes 3000000 | tf_op jit(solution)/shard_map/combine/pallas_call | solution.py:207
  39.9 12.5 %all_to_all.10.sum_ref = bf16[16,11,8,128]{3,2,1,0:T(8,128)(2,1)S(1)} all-to-all(bf16[16,11,8,128]{3,2,1,0:T(8,128)(2,1)S(1)} %combine.1), channel_id=1, replica_groups=mesh['pair'=8,'aux'=16] {'aux'}, dimensions={0} | all-to-all | bytes 720896 | tf_op jit(solution)/shard_map/all_to_all | solution.py:222
  52.3 0.0 copy-done.4
  52.4 0.0 copy-done.5
  52.4 1.4 %finish.1 = (f32[10,8,128]{2,1,0:T(8,128)}, f32[3,4,48]{2,1,0:T(4,128)}) custom-call(bf16[16,11,8,128]{3,2,1,0:T(8,128)(2,1)S(1)} %all_to_all.10.sum_ref, bf16[10,8,128]{2,1,0:T(8,128)(2,1)S(1)} %copy-done.4, s32[10]{0:T(128)S(1)} %copy-done.8, f32[10]{0:T(128)S(1)} %copy-done.10, f32[10,128]{1,0:T(8,128)S(1)} %copy-done.6, bf16[3,4,48]{2,1,0:T(4,128)(2,1)S(1)} %bitcast.5, ...), custom_call_target="tpu_custom_call" | custom-call | flops 1000000 | bytes 1000000 | tf_op jit(solution)/shard_map/finish/pallas_call | solution.py:223
  (14 shorter events, 0.0 us)
Async XLA Ops:
  2.2 33.0 %collective-permute-start.3 = (bf16[14,8,128]{2,1,0:T(8,128)(2,1)}, bf16[14,8,128]{2,1,0:T(8,128)(2,1)S(1)}, u32[]{:S(2)}, u32[]{:S(2)}) collective-permute-start(bf16[14,8,128]{2,1,0:T(8,128)(2,1)} %get-tuple-element.9.block_ref.refs_0_), channel_id=1, source_target_pairs={{0,16},{16,0},{32,48},{48,32},{64,80},{80,64},{96,112},{112,96},{1... | collective-permute-start | bytes 86024 | tf_op jit(solution)/shard_map/ppermute | solution.py:197
  2.2 13.4 %collective-permute-start.2 = (bf16[14,8,128]{2,1,0:T(8,128)(2,1)}, bf16[14,8,128]{2,1,0:T(8,128)(2,1)}, u32[]{:S(2)}, u32[]{:S(2)}) collective-permute-start(bf16[14,8,128]{2,1,0:T(8,128)(2,1)} %get-tuple-element.9.block_ref.refs_0_), channel_id=1, source_target_pairs={{0,96},{16,112},{32,0},{48,16},{64,32},{80,48},{96,64},{112,80},{1... | collective-permute-start | bytes 86024 | tf_op jit(solution)/shard_map/ppermute | solution.py:194
  5.1 10.7 %collective-permute-start.1 = (bf16[14,8,128]{2,1,0:T(8,128)(2,1)}, bf16[14,8,128]{2,1,0:T(8,128)(2,1)}, u32[]{:S(2)}, u32[]{:S(2)}) collective-permute-start(bf16[14,8,128]{2,1,0:T(8,128)(2,1)} %get-tuple-element.9.block_ref.refs_0_), channel_id=1, source_target_pairs={{0,64},{16,80},{32,96},{48,112},{64,0},{80,16},{96,32},{112,48},{1... | collective-permute-start | bytes 86024 | tf_op jit(solution)/shard_map/ppermute | solution.py:194
  5.9 10.4 %collective-permute-start = (bf16[14,8,128]{2,1,0:T(8,128)(2,1)}, bf16[14,8,128]{2,1,0:T(8,128)(2,1)}, u32[]{:S(2)}, u32[]{:S(2)}) collective-permute-start(bf16[14,8,128]{2,1,0:T(8,128)(2,1)} %get-tuple-element.9.block_ref.refs_0_), channel_id=1, source_target_pairs={{0,32},{16,48},{32,64},{48,80},{64,96},{80,112},{96,0},{112,16},{1... | collective-permute-start | bytes 86024 | tf_op jit(solution)/shard_map/ppermute | solution.py:194
  6.8 17.1 %all-to-all-start = ((bf16[16,10,8,128]{3,2,1,0:T(8,128)(2,1)}), bf16[16,10,8,128]{3,2,1,0:T(8,128)(2,1)S(1)}, u32[]{:S(2)}, u32[]{:S(2)}) async-start(bf16[16,10,8,128]{3,2,1,0:T(8,128)(2,1)} %get-tuple-element.8), calls=%async_computation | async-start | bytes 655360 | tf_op jit(solution)/shard_map/all_to_all | solution.py:195
  14.8 0.8 %copy-start.14 = (bf16[14,8,128]{2,1,0:T(8,128)(2,1)S(1)}, bf16[14,8,128]{2,1,0:T(8,128)(2,1)}, u32[]{:S(2)}) copy-start(bf16[14,8,128]{2,1,0:T(8,128)(2,1)} %get-tuple-element.9.block_ref.refs_0_) | copy-start | bytes 86020
  15.6 8.2 %copy-start.2 = (bf16[4,48,3840]{2,1,0:T(8,128)(2,1)S(1)}, bf16[4,48,3840]{2,1,0:T(8,128)(2,1)}, u32[]{:S(2)}) copy-start(bf16[4,48,3840]{2,1,0:T(8,128)(2,1)} %le_ref.1) | copy-start | bytes 4423684
  15.6 8.2 %copy-start.3 = (bf16[4,48,3840]{2,1,0:T(8,128)(2,1)S(1)}, bf16[4,48,3840]{2,1,0:T(8,128)(2,1)}, u32[]{:S(2)}) copy-start(bf16[4,48,3840]{2,1,0:T(8,128)(2,1)} %re_ref.2) | copy-start | bytes 4423684
  15.6 19.7 %copy-start.13 = (bf16[4,4,48,48]{3,2,1,0:T(8,128)(2,1)S(1)}, bf16[4,4,48,48]{3,2,1,0:T(8,128)(2,1)}, u32[]{:S(2)}) copy-start(bf16[4,4,48,48]{3,2,1,0:T(8,128)(2,1)} %refs_9_.1) | copy-start | bytes 221188
  15.6 19.7 %copy-start.15 = (bf16[14,8,128]{2,1,0:T(8,128)(2,1)S(1)}, bf16[14,8,128]{2,1,0:T(8,128)(2,1)}, u32[]{:S(2)}) copy-start(bf16[14,8,128]{2,1,0:T(8,128)(2,1)} %get-tuple-element.9.block_ref.refs_0_) | copy-start | bytes 86020
  15.6 19.7 %copy-start.16 = (f32[10,4]{0,1:T(4,128)S(1)}, f32[10,4]{0,1:T(4,128)}, u32[]{:S(2)}) copy-start(f32[10,4]{0,1:T(4,128)} %param.25) | copy-start | bytes 484
  15.6 19.7 %copy-start.17 = (s32[10,4]{0,1:T(4,128)S(1)}, s32[10,4]{0,1:T(4,128)}, u32[]{:S(2)}) copy-start(s32[10,4]{0,1:T(4,128)} %param.26) | copy-start | bytes 484
  15.6 19.7 %copy-start.18 = (f32[4,4]{1,0:T(4,128)S(1)}, f32[4,4]{1,0:T(4,128)}, u32[]{:S(2)}) copy-start(f32[4,4]{1,0:T(4,128)} %refs_12_.1) | copy-start | bytes 196
  15.6 19.7 %copy-start.19 = (s32[4,4]{1,0:T(4,128)S(1)}, s32[4,4]{1,0:T(4,128)}, u32[]{:S(2)}) copy-start(s32[4,4]{1,0:T(4,128)} %refs_13_.1) | copy-start | bytes 196
  15.7 19.6 %collective-permute-start.6 = (bf16[14,8,128]{2,1,0:T(8,128)(2,1)}, bf16[14,8,128]{2,1,0:T(8,128)(2,1)}, u32[]{:S(2)}, u32[]{:S(2)}) collective-permute-start(bf16[14,8,128]{2,1,0:T(8,128)(2,1)} %collective-permute-done.2.refs_3_), channel_id=1, source_target_pairs={{0,16},{16,0},{32,48},{48,32},{64,80},{80,64},{96,112},{112,96},{1... | collective-permute-start | bytes 86024 | tf_op jit(solution)/shard_map/ppermute | solution.py:197
  15.8 19.5 %collective-permute-start.5 = (bf16[14,8,128]{2,1,0:T(8,128)(2,1)}, bf16[14,8,128]{2,1,0:T(8,128)(2,1)}, u32[]{:S(2)}, u32[]{:S(2)}) collective-permute-start(bf16[14,8,128]{2,1,0:T(8,128)(2,1)} %collective-permute-done.1.refs_2_), channel_id=1, source_target_pairs={{0,16},{16,0},{32,48},{48,32},{64,80},{80,64},{96,112},{112,96},{1... | collective-permute-start | bytes 86024 | tf_op jit(solution)/shard_map/ppermute | solution.py:197
  16.3 19.0 %collective-permute-start.4 = (bf16[14,8,128]{2,1,0:T(8,128)(2,1)}, bf16[14,8,128]{2,1,0:T(8,128)(2,1)}, u32[]{:S(2)}, u32[]{:S(2)}) collective-permute-start(bf16[14,8,128]{2,1,0:T(8,128)(2,1)} %collective-permute-done.refs_1_), channel_id=1, source_target_pairs={{0,16},{16,0},{32,48},{48,32},{64,80},{80,64},{96,112},{112,96},{1... | collective-permute-start | bytes 86024 | tf_op jit(solution)/shard_map/ppermute | solution.py:197
  23.8 3.8 %copy-start = (bf16[10,128,3840]{2,1,0:T(8,128)(2,1)S(1)}, bf16[10,128,3840]{2,1,0:T(8,128)(2,1)}, u32[]{:S(2)}) copy-start(bf16[10,128,3840]{2,1,0:T(8,128)(2,1)} %la_ref.1) | copy-start | bytes 29491204
  27.6 3.8 %copy-start.1 = (bf16[10,128,3840]{2,1,0:T(8,128)(2,1)S(1)}, bf16[10,128,3840]{2,1,0:T(8,128)(2,1)}, u32[]{:S(2)}) copy-start(bf16[10,128,3840]{2,1,0:T(8,128)(2,1)} %ra_ref.2) | copy-start | bytes 29491204
  31.4 3.9 %copy-start.12 = (bf16[10,4,128,128]{3,2,1,0:T(8,128)(2,1)S(1)}, bf16[10,4,128,128]{3,2,1,0:T(8,128)(2,1)}, u32[]{:S(2)}) copy-start(bf16[10,4,128,128]{3,2,1,0:T(8,128)(2,1)} %refs_8_.1) | copy-start | bytes 3932164
  35.4 17.0 %copy-start.4 = (bf16[10,8,128]{2,1,0:T(8,128)(2,1)S(1)}, bf16[10,8,128]{2,1,0:T(8,128)(2,1)}, u32[]{:S(2)}) copy-start(bf16[10,8,128]{2,1,0:T(8,128)(2,1)} %aa_ref.1) | copy-start | bytes 61444
  35.4 17.0 %copy-start.5 = (bf16[4,3,48]{2,0,1:T(4,128)(2,1)S(1)}, bf16[4,3,48]{2,0,1:T(4,128)(2,1)}, u32[]{:S(2)}) copy-start(bf16[4,3,48]{2,0,1:T(4,128)(2,1)} %param.29) | copy-start | bytes 3460
  35.4 17.0 %copy-start.6 = (f32[10,128]{1,0:T(8,128)S(1)}, f32[10,128]{1,0:T(8,128)}, u32[]{:S(2)}) copy-start(f32[10,128]{1,0:T(8,128)} %ea_ref.1) | copy-start | bytes 15364
  35.4 17.0 %copy-start.7 = (f32[4,48]{1,0:T(4,128)S(1)}, f32[4,48]{1,0:T(4,128)}, u32[]{:S(2)}) copy-start(f32[4,48]{1,0:T(4,128)} %ee_ref.1) | copy-start | bytes 2308
  35.4 17.0 %copy-start.8 = (s32[10]{0:T(128)S(1)}, s32[10]{0:T(128)}, u32[]{:S(2)}) copy-start(s32[10]{0:T(128)} %ra_ref.3) | copy-start | bytes 124
  35.4 17.0 %copy-start.9 = (s32[4]{0:T(128)S(1)}, s32[4]{0:T(128)}, u32[]{:S(2)}) copy-start(s32[4]{0:T(128)} %re_ref.3) | copy-start | bytes 52
  35.4 17.0 %copy-start.10 = (f32[10]{0:T(128)S(1)}, f32[10]{0:T(128)}, u32[]{:S(2)}) copy-start(f32[10]{0:T(128)} %ga_ref.1) | copy-start | bytes 124
  35.4 17.0 %copy-start.11 = (f32[4]{0:T(128)S(1)}, f32[4]{0:T(128)}, u32[]{:S(2)}) copy-start(f32[4]{0:T(128)} %ge_ref.1) | copy-start | bytes 52

commit v3 on v2

v3 whole, which is shorter than its diff:
```python
import jax
import jax.numpy as jnp
from jax import lax
from jax.experimental import pallas as pl
from jax.experimental.pallas import tpu as pltpu
from jax.sharding import PartitionSpec as P


BF16 = jnp.bfloat16
F32 = jnp.float32
VMEM = pl.BlockSpec(memory_space=pltpu.VMEM)
SMEM = pl.BlockSpec(memory_space=pltpu.SMEM)
HBM = pl.BlockSpec(memory_space=pl.ANY)
MARK = 3 * 10**10
BIG = pltpu.CompilerParams(vmem_limit_bytes=60 * 1024 * 1024)
SMALL = pltpu.CompilerParams(vmem_limit_bytes=8 * 1024 * 1024)


def dot(left, right, contract):
    return lax.dot_general(left, right, ((contract[:1], contract[1:]), ((), ())), preferred_element_type=F32)


def dot_nt(left, right):
    return dot(left, right, (1, 1))


def dot_nn(left, right):
    return dot(left, right, (1, 0))


def dot_tn(left, right):
    return dot(left, right, (0, 0))


def own_energies(energy, shape, start):
    row = lax.broadcasted_iota(jnp.int32, shape, 0)
    col = lax.broadcasted_iota(jnp.int32, shape, 1)
    return jnp.sum(jnp.where(col == start + row, energy, 0.0), axis=1, keepdims=True)


def inside(shape, rank, start):
    rows = start + lax.broadcasted_iota(jnp.int32, shape, 0)
    return (rows < rank) & (lax.broadcasted_iota(jnp.int32, shape, 1) < rank)


def pack_kernel(
    aa_ref, ra_ref, ga_ref, ea_ref, ae_ref, re_ref, ge_ref, ee_ref, block_ref, scale_a_ref, scale_e_ref
):
    place = lax.axis_index("aux")
    n_act, rows_act, _ = aa_ref.shape
    rows_env, n_env, width_env = ae_ref.shape

    def prepare(amps, rank, gap, energy, start):
        keep = inside(amps.shape, rank, start)
        scale = 1.0 / (own_energies(energy, amps.shape, start) + energy + gap)
        return jnp.where(keep, amps.astype(F32), 0.0).astype(BF16), jnp.where(keep, scale, 0.0)

    for p in range(n_act):
        block_ref[p], scale_a_ref[p] = prepare(
            aa_ref[p], ra_ref[p], ga_ref[p], ea_ref[p : p + 1], place * rows_act
        )
    block_ref[n_act:] = jnp.zeros((n_env, 8, 128), BF16)
    for p in range(n_env):
        block_ref[n_act + p, 0:rows_env, 0:width_env], scale_e_ref[:, p] = prepare(
            ae_ref[:, p], re_ref[p], ge_ref[p], ee_ref[p : p + 1], place * rows_env
        )


def mark_kernel(_, mark_ref):
    mark_ref[...] = jnp.zeros(mark_ref.shape, F32)


def stack_kernel(*refs):
    for i, ref in enumerate(refs[:-1]):
        refs[-1][i] = ref[0 : refs[-1].shape[1]]


def main_kernel(la_ref, ra_ref, le_ref, re_ref, mark_ref, *refs):
    n_near = len(refs) - 15
    near_refs = refs[:n_near]
    xa_ref, xe_ref, *tables, sa_ref, ca_ref, se_ref, near_ref = refs[n_near : n_near + 10]
    fa_ref, na_ref, fe_ref, ne_ref, sems = refs[n_near + 10 :]
    copies = [
        pltpu.make_async_copy(source, target, sems.at[i])
        for i, (source, target) in enumerate(zip(tables, (fa_ref, na_ref, fe_ref, ne_ref)))
    ]
    for copy in copies:
        copy.start()
    place, group = lax.axis_index("aux"), lax.axis_index("pair")
    n_act, width, _ = sa_ref.shape
    n_env, width_env, _ = se_ref.shape
    rows_env = width_env // (width // 8)
    for slot in range(n_near):
        near_ref[slot] = near_refs[slot][...]
    for p in range(n_act):
        sa_ref[p] = dot_nt(la_ref[p], ra_ref[p])
    for p in range(n_env):
        se_ref[p] = dot_nt(le_ref[p], re_ref[p])
    for copy in copies:
        copy.wait()

    def near_block(n, count, first):
        source = n // count
        slot = (group // 2 + n_near - source // 2) % n_near
        return near_ref[slot, (group + source) % 2, first + n % count]

    lane = lax.broadcasted_iota(jnp.int32, (width, width), 1) // 8
    for p in range(n_act):
        halves, cols = [], jnp.zeros((width, width), F32)
        for k in range(4):
            near = near_block(na_ref[k, p], n_act, 0)
            halves.append(dot_nt(near, xa_ref[p, k]) * fa_ref[k, p])
            turned = pltpu.roll(xa_ref[p, k].astype(F32), (width + 8 * k - 8 * place) % width, 1)
            cols = jnp.where(lane == k, turned, cols)
        halves.append(jnp.zeros((width - 32, width), F32))
        ca_ref[p] = dot_nn(cols.astype(BF16), jnp.concatenate(halves, axis=0).astype(BF16))
    row = lax.broadcasted_iota(jnp.int32, (width_env, 8), 0)
    col = lax.broadcasted_iota(jnp.int32, (width_env, 8), 1)
    pick = jnp.where((row == place * rows_env + col) & (col < rows_env), 1.0, 0.0).astype(BF16)
    for p in range(n_env):
        total = se_ref[p]
        for k in range(4):
            near = near_block(ne_ref[p, k], n_env, n_act)[:, 0:width_env]
            half = dot_nt(near, xe_ref[p, k]) * fe_ref[p, k]
            cols = dot_nn(xe_ref[p, k], pick)
            total = total + dot_nn(cols.astype(BF16), half.astype(BF16))
        se_ref[p] = total


def combine_kernel(sa_ref, ca_ref, se_ref, *refs):
    own_refs, (out_ref, own_ref) = refs[:-2], refs[-2:]
    place = lax.axis_index("aux")
    n_own = len(own_refs)
    n_aux, (n_act, width, _) = out_ref.shape[0], sa_ref.shape
    n_env, width_env, _ = se_ref.shape
    rows_env = width_env // n_aux
    side = own_refs[0].shape[0]
    for dz in range(n_own):
        for dy in range(side):
            y = (place // n_own + side - dy) % side
            own_ref[y * n_own + (place + n_own - dz) % n_own] = own_refs[dz][dy]
    for p in range(n_act):
        amps = own_ref[:, p].reshape(width, width)
        base = sa_ref[p]
        once = dot_tn(amps, base.astype(BF16))
        twice = dot_nt(once.astype(BF16), amps)
        total = base + once + twice + ca_ref[p]
        out_ref[:, p] = total.astype(BF16).reshape(n_aux, 8, width)
    env = [se_ref[p].astype(BF16) for p in range(n_env)]
    row = lax.broadcasted_iota(jnp.int32, (n_aux * 8, 2 * width_env), 0)
    col = lax.broadcasted_iota(jnp.int32, (n_aux * 8, 2 * width_env), 1)
    slot = row % 8
    source = jnp.where(slot < rows_env, slot, width_env + slot - rows_env) + rows_env * (row // 8)
    spread = jnp.where((col == source) & (slot < 2 * rows_env), 1.0, 0.0).astype(BF16)
    out_ref[:, n_act] = jnp.zeros((n_aux, 8, width), BF16)
    for half in range(2):
        both = jnp.concatenate([env[2 * half], env[2 * half + 1]], axis=0)
        laid = dot_nn(spread, both).astype(BF16).reshape(n_aux, 8, width_env)
        out_ref[:, n_act, :, 64 * half : 64 * half + width_env] = laid


def finish_kernel(sum_ref, block_ref, scale_a_ref, scale_e_ref, oa_ref, oe_ref):
    n_act = scale_a_ref.shape[0]
    rows_env, n_env, width_env = scale_e_ref.shape
    for p in range(n_act):
        summed = jnp.sum(sum_ref[:, p].astype(F32), axis=0)
        oa_ref[p] = block_ref[p].astype(F32) - summed * scale_a_ref[p]
    summed = jnp.sum(sum_ref[:, n_act].astype(F32), axis=0)
    for p in range(n_env):
        half, at = p // 2, rows_env * (p % 2)
        mine = summed[at : at + rows_env, 64 * half : 64 * half + width_env]
        amps = block_ref[n_act + p, 0:rows_env, 0:width_env].astype(F32)
        oe_ref[:, p] = amps - mine * scale_e_ref[:, p]


def shards(
    left_active, right_active, amps_active, rank_active, gap_active, energy_active,
    intersect_active, fock_active, neighbor_active,
    left_env, right_env, amps_env, rank_env, gap_env, energy_env,
    intersect_env, fock_env, neighbor_env,
):
    n_act, rows_act, width = amps_active.shape
    n_env, rows_env, width_env = amps_env.shape
    n_aux, n_pair, n_z = lax.axis_size("aux"), lax.axis_size("pair"), 4
    shape = jax.ShapeDtypeStruct

    def call(kernel, out, ins, *arrays, scratch=(), params=SMALL, flops=10**6):
        return pl.pallas_call(
            kernel,
            out_shape=out,
            in_specs=ins,
            out_specs=jax.tree.map(lambda _: VMEM, out),
            scratch_shapes=scratch,
            compiler_params=params,
            cost_estimate=pl.CostEstimate(flops=flops, bytes_accessed=10**6, transcendentals=0),
        )(*arrays)

    def moved(x, axis, size, route):
        return lax.ppermute(x, axis, [(i, route(i)) for i in range(size)])

    def stack(arrays, tiles):
        out = shape((len(arrays), tiles, 8, 128), BF16)
        return call(stack_kernel, out, [VMEM] * len(arrays), *arrays)

    block, scale_act, scale_env = call(
        pack_kernel,
        [
            shape((n_act + n_env, 8, 128), BF16),
            shape((n_act, rows_act, width), F32),
            shape((rows_env, n_env, width_env), F32),
        ],
        [VMEM, SMEM, SMEM, VMEM] * 2,
        amps_active, rank_active, gap_active, energy_active,
        amps_env.transpose(1, 0, 2), rank_env, gap_env, energy_env,
        params=BIG,
    )
    mark = call(mark_kernel, shape((8, 128), F32), [HBM], block, flops=MARK)
    other = moved(block, "pair", n_pair, lambda i: i ^ 1)
    own = [block]
    for step in range(1, n_aux // n_z):
        own.append(moved(block, "aux", n_aux, lambda i: (i + n_z * step) % n_aux))
    near = [stack([block, other], n_act + n_env)]
    for step in range(1, n_pair // 2):
        near.append(moved(near[0], "pair", n_pair, lambda i: (i + 2 * step) % n_pair))
    own = [stack(own, n_act)]
    for step in range(1, n_z):
        own.append(moved(own[0], "aux", n_aux, lambda i: i // n_z * n_z + (i + step) % n_z))
    sum_act, couple_act, sum_env = call(
        main_kernel,
        [shape((n_act, width, width), F32)] * 2 + [shape((n_env, width_env, width_env), F32)],
        [VMEM] * 4 + [HBM] + [VMEM] * (len(near) + 2) + [HBM] * 4,
        left_active, right_active, left_env, right_env, mark,
        *near, intersect_active, intersect_env, fock_active.T, neighbor_active.T, fock_env, neighbor_env,
        scratch=[
            pltpu.VMEM((len(near), 2, n_act + n_env, 8, 128), BF16),
            pltpu.SMEM((4, n_act), F32),
            pltpu.SMEM((4, n_act), jnp.int32),
            pltpu.SMEM((n_env, 4), F32),
            pltpu.SMEM((n_env, 4), jnp.int32),
            pltpu.SemaphoreType.DMA((4,)),
        ],
        flops=5 * 10**9,
    )
    shares = call(
        combine_kernel, shape((n_aux, n_act + 1, 8, 128), BF16), [VMEM] * (3 + len(own)),
        sum_act, couple_act, sum_env, *own,
        scratch=[pltpu.VMEM((n_aux, n_act, 8, 128), BF16)], flops=10**9,
    )
    summed = lax.all_to_all(shares, "aux", 0, 0, tiled=True)
    new_active, new_env = call(
        finish_kernel,
        [shape((n_act, rows_act, width), F32), shape((rows_env, n_env, width_env), F32)],
        [VMEM] * 4,
        summed, block, scale_act, scale_env,
    )
    return new_active, new_env.transpose(1, 0, 2)


def solution(mesh):
    rows = P("pair", "aux", None)
    deep = P("pair", None, "aux")
    per_pair = P("pair")
    level = (
        deep, deep, rows, per_pair, per_pair, P("pair", None),
        P("pair", None, None, None), P("pair", None), P("pair", None),
    )

    return jax.shard_map(
        shards, mesh=mesh, in_specs=level + level, out_specs=(rows, rows), check_vma=False
    )
```

time: 54.5 us -> 41.7 us (0.77)
  local copies, waits for them, and re-layouts: 8.43 us -> 0.88 us
  waiting for transfers between devices: 7.48 us -> 0.03 us
  blocking collectives: 12.5 us -> 15.1 us
  starting transfers between devices: 13.3 us -> 14.6 us
  Pallas kernels: 11.2 us -> 9.91 us
    ppermute x7 -> x10, starting transfers between devices: 5.24 us -> 14.6 us  [moved(): return lax.ppermute(x, axis, [(i, route(i)) for i in range(size)])]
    all_to_all x1 -> x0, starting transfers between devices: 8.05 us -> none  [shards(): own = lax.all_to_all(for_aux, 'aux', 0, 0, tiled=True)]
    unnamed x40 -> x36, local copies, waits for them, and re-layouts: 8.43 us -> 0.88 us
    all_to_all x1 -> x0, waiting for transfers between devices: 7.46 us -> none  [shards(): own = lax.all_to_all(for_aux, 'aux', 0, 0, tiled=True)]
    all_to_all x1, blocking collectives: 12.5 us -> 15.1 us  [shards(): summed = lax.all_to_all(shares, 'aux', 0, 0, tiled=True)]
    pallas_call x5 -> x7, Pallas kernels: 11.2 us -> 9.91 us  [call(): pl.pallas_call(kernel, out_shape=out, in_specs=ins, out_specs=jax.tree.ma...]
  transfers between devices with their start and end apart: 8 -> 10, of which waited for: 1 -> 0; matrix products, arithmetic and copies ran while one was open for 0% -> 0% of each run, Pallas kernels for 7% -> 16%
where the time goes in v3:
time: 41.7 us; the launch traced here: 41.5 us
  blocking collectives  15.1 us (36%)
  starting transfers between devices  14.6 us (35%)
  Pallas kernels  9.91 us (24%)
  between operations  0.94 us (2%)
  local copies, waits for them, and re-layouts  0.88 us (2%)
    all_to_all x1, blocking collectives, shards(): summed = lax.all_to_all(shares, 'aux', 0, 0, tiled=True)  15.1 us
    ppermute x10, starting transfers between devices, moved(): return lax.ppermute(x, axis, [(i, route(i)) for i in range(size)])  14.6 us
    pallas_call x7, Pallas kernels, call(): pl.pallas_call(kernel, out_shape=out, in_specs=ins, out_specs=jax.tree.ma...  9.91 us
    unnamed x36, local copies, waits for them, and re-layouts  0.88 us
  transfers between devices with their start and end apart: 10, of which 0 were waited for; matrix products, arithmetic and copies ran while one was open for 0% of the time, Pallas kernels for 16%

profile of v3, /device:TPU:0, one launch (start us, length us, event | category | flops | bytes accessed | tf_op | source)
XLA Modules:
  0.0 41.5 jit_solution(5321782727818014664)
XLA Ops:
  0.6 1.6 %shard_map.185 = (bf16[14,8,128]{2,1,0:T(8,128)(2,1)}, f32[10,8,128]{2,1,0:T(8,128)}, f32[3,4,48]{2,1,0:T(4,128)}) custom-call(bf16[10,8,128]{2,1,0:T(8,128)(2,1)} %aa_ref.1, s32[10]{0:T(128)} %ra_ref.2, f32[10]{0:T(128)} %ga_ref.1, f32[10,128]{1,0:T(8,128)} %ea_ref.1, bf16[3,4,48]{2,1,0:T(4,128)(2,1)} %bitcast.10, s32[4]{0:T(128)} %re_ref.2, f32[4]{0:T(128)} %ge_ref.1, ...), custom_call_target="tpu_custom_call" | custom-call | flops 1000000 | bytes 1000000 | tf_op jit(solution)/shard_map/pallas_call | solution.py:188
  2.2 0.0 collective-permute-start
  2.2 3.2 %collective-permute-start.6 = (bf16[14,8,128]{2,1,0:T(8,128)(2,1)}, bf16[14,8,128]{2,1,0:T(8,128)(2,1)S(1)}, u32[]{:S(2)}, u32[]{:S(2)}) collective-permute-start(bf16[14,8,128]{2,1,0:T(8,128)(2,1)} %get-tuple-element.10._.refs_0_.block_ref), channel_id=1, source_target_pairs={{0,12},{1,13},{2,14},{3,15},{4,0},{5,1},{6,2},{7,3},{8,4},{9,5},{1... | collective-permute-start | bytes 86024 | tf_op jit(solution)/shard_map/ppermute | solution.py:199
  5.3 0.6 %collective-permute-start.5 = (bf16[14,8,128]{2,1,0:T(8,128)(2,1)}, bf16[14,8,128]{2,1,0:T(8,128)(2,1)S(1)}, u32[]{:S(2)}, u32[]{:S(2)}) collective-permute-start(bf16[14,8,128]{2,1,0:T(8,128)(2,1)} %get-tuple-element.10._.refs_0_.block_ref), channel_id=1, source_target_pairs={{0,8},{1,9},{2,10},{3,11},{4,12},{5,13},{6,14},{7,15},{8,0},{9,1},... | collective-permute-start | bytes 86024 | tf_op jit(solution)/shard_map/ppermute | solution.py:199
  6.0 1.0 %collective-permute-start.4 = (bf16[14,8,128]{2,1,0:T(8,128)(2,1)}, bf16[14,8,128]{2,1,0:T(8,128)(2,1)S(1)}, u32[]{:S(2)}, u32[]{:S(2)}) collective-permute-start(bf16[14,8,128]{2,1,0:T(8,128)(2,1)} %get-tuple-element.10._.refs_0_.block_ref), channel_id=1, source_target_pairs={{0,4},{1,5},{2,6},{3,7},{4,8},{5,9},{6,10},{7,11},{8,12},{9,13},{1... | collective-permute-start | bytes 86024 | tf_op jit(solution)/shard_map/ppermute | solution.py:199
  6.9 0.0 collective-permute-done.refs_1_
  6.9 0.8 %copy-done.3 = bf16[14,8,128]{2,1,0:T(8,128)(2,1)S(1)} copy-done((bf16[14,8,128]{2,1,0:T(8,128)(2,1)S(1)}, bf16[14,8,128]{2,1,0:T(8,128)(2,1)}, u32[]{:S(2)}) %copy-start.3) | copy-done | bytes 28696
  7.7 0.0 slice-start.1
  7.8 0.0 slice-start.2
  7.8 0.0 slice-start.4
  7.8 0.0 slice-start.5
  7.8 0.0 copy-start
  7.8 0.0 copy-start.1
  7.8 0.0 copy-start.2
  7.8 0.0 copy-start.5
  7.8 0.0 copy-start.8
  7.8 0.0 copy-start.9
  7.9 0.0 copy-start.10
  7.9 0.0 copy-start.11
  7.9 2.8 %collective-permute-start.3 = (bf16[2,14,8,128]{3,2,1,0:T(8,128)(2,1)S(1)}, bf16[2,14,8,128]{3,2,1,0:T(8,128)(2,1)S(1)}, u32[]{:S(2)}, u32[]{:S(2)}) collective-permute-start(bf16[2,14,8,128]{3,2,1,0:T(8,128)(2,1)S(1)} %shard_map.187.refs_0_), channel_id=1, source_target_pairs={{0,96},{16,112},{32,0},{48,16},{64,32},{80,48},{96,64},{112,80},{1... | collective-permute-start | bytes 172040 | tf_op jit(solution)/shard_map/ppermute | solution.py:199
  10.7 0.8 %collective-permute-start.2 = (bf16[2,14,8,128]{3,2,1,0:T(8,128)(2,1)S(1)}, bf16[2,14,8,128]{3,2,1,0:T(8,128)(2,1)S(1)}, u32[]{:S(2)}, u32[]{:S(2)}) collective-permute-start(bf16[2,14,8,128]{3,2,1,0:T(8,128)(2,1)S(1)} %shard_map.187.refs_0_), channel_id=1, source_target_pairs={{0,64},{16,80},{32,96},{48,112},{64,0},{80,16},{96,32},{112,48},{1... | collective-permute-start | bytes 172040 | tf_op jit(solution)/shard_map/ppermute | solution.py:199
  11.5 0.0 collective-permute-done.6.refs_3_
  11.5 0.9 %collective-permute-start.1 = (bf16[2,14,8,128]{3,2,1,0:T(8,128)(2,1)S(1)}, bf16[2,14,8,128]{3,2,1,0:T(8,128)(2,1)S(1)}, u32[]{:S(2)}, u32[]{:S(2)}) collective-permute-start(bf16[2,14,8,128]{3,2,1,0:T(8,128)(2,1)S(1)} %shard_map.187.refs_0_), channel_id=1, source_target_pairs={{0,32},{16,48},{32,64},{48,80},{64,96},{80,112},{96,0},{112,16},{1... | collective-permute-start | bytes 172040 | tf_op jit(solution)/shard_map/ppermute | solution.py:199
  12.4 0.0 collective-permute-done.5.refs_2_
  12.4 0.0 collective-permute-done.4.refs_1_
  12.4 4.1 %collective-permute-start.9 = (bf16[4,10,8,128]{3,2,1,0:T(8,128)(2,1)S(1)}, bf16[4,10,8,128]{3,2,1,0:T(8,128)(2,1)S(1)}, u32[]{:S(2)}, u32[]{:S(2)}) collective-permute-start(bf16[4,10,8,128]{3,2,1,0:T(8,128)(2,1)S(1)} %shard_map.189.refs_0_), channel_id=1, source_target_pairs={{0,3},{1,0},{2,1},{3,2},{4,7},{5,4},{6,5},{7,6},{8,11},{9,8},{10,9... | collective-permute-start | bytes 245768 | tf_op jit(solution)/shard_map/ppermute | solution.py:199
  16.5 0.0 collective-permute-start.8
  16.5 0.0 collective-permute-done.3.refs_3_
  16.5 1.3 %collective-permute-start.7 = (bf16[4,10,8,128]{3,2,1,0:T(8,128)(2,1)S(1)}, bf16[4,10,8,128]{3,2,1,0:T(8,128)(2,1)S(1)}, u32[]{:S(2)}, u32[]{:S(2)}) collective-permute-start(bf16[4,10,8,128]{3,2,1,0:T(8,128)(2,1)S(1)} %shard_map.189.refs_0_), channel_id=1, source_target_pairs={{0,1},{1,2},{2,3},{3,0},{4,5},{5,6},{6,7},{7,4},{8,9},{9,10},{10,1... | collective-permute-start | bytes 245768 | tf_op jit(solution)/shard_map/ppermute | solution.py:199
  17.8 0.0 collective-permute-done.2.refs_2_
  17.8 0.0 collective-permute-done.1.refs_1_
  17.8 0.0 slice-done
  17.8 0.0 slice-done.3
  17.8 0.0 slice-done.1
  17.8 0.0 slice-done.2
  17.8 0.0 slice-done.4
  17.9 0.0 slice-done.5
  18.0 6.6 %shard_map.188 = (f32[10,128,128]{2,1,0:T(8,128)S(1)}, f32[10,128,128]{2,1,0:T(8,128)S(1)}, f32[4,48,48]{2,1,0:T(8,128)S(1)}) custom-call(bf16[10,128,3840]{2,1,0:T(8,128)(2,1)S(1)} %bitcast.5, bf16[10,128,3840]{2,1,0:T(8,128)(2,1)S(1)} %bitcast.7, bf16[4,48,3840]{2,1,0:T(8,128)(2,1)S(1)} %copy-done, bf16[4,48,3840]{2,1,0:T(8,128)(2,1)S(1)} %copy-done.1, ...), custom_call_target="tpu_custom_call" | custom-call | flops 5000000000 | bytes 1000000 | tf_op jit(solution)/shard_map/pallas_call | solution.py:188
  24.5 0.0 collective-permute-done.9.refs_3_
  24.5 0.0 collective-permute-done.8.refs_2_
  24.6 0.0 collective-permute-done.7.refs_1_
  24.6 0.0 copy-start.4
  24.6 0.0 copy-start.6
  24.6 0.0 copy-start.7
  24.6 1.0 %shard_map.190 = bf16[16,11,8,128]{3,2,1,0:T(8,128)(2,1)S(1)} custom-call(f32[10,128,128]{2,1,0:T(8,128)S(1)} %get-tuple-element.11.sa_ref, f32[10,128,128]{2,1,0:T(8,128)S(1)} %get-tuple-element.12.ca_ref, f32[4,48,48]{2,1,0:T(8,128)S(1)} %get-tuple-element.13.se_ref, bf16[4,10,8,128]{3,2,1,0:T(8,128)(2,1)S(1)} %shard_map.189.refs_0_, ...), custom_call_target="tpu_custom_call" | custom-call | flops 1000000000 | bytes 1000000 | tf_op jit(solution)/shard_map/pallas_call | solution.py:188
  25.6 15.1 %all_to_all.5.sum_ref = bf16[16,11,8,128]{3,2,1,0:T(8,128)(2,1)S(1)} all-to-all(bf16[16,11,8,128]{3,2,1,0:T(8,128)(2,1)S(1)} %shard_map.190), channel_id=1, replica_groups=mesh['pair'=8,'aux'=16] {'aux'}, dimensions={0} | all-to-all | bytes 720896 | tf_op jit(solution)/shard_map/all_to_all | solution.py:249
  40.7 0.0 copy-done.6
  40.7 0.7 %shard_map.191 = (f32[10,8,128]{2,1,0:T(8,128)}, f32[3,4,48]{2,1,0:T(4,128)}) custom-call(bf16[16,11,8,128]{3,2,1,0:T(8,128)(2,1)S(1)} %all_to_all.5.sum_ref, bf16[14,8,128]{2,1,0:T(8,128)(2,1)S(1)} %copy-done.4, f32[10,8,128]{2,1,0:T(8,128)S(1)} %copy-done.6, f32[3,4,48]{2,1,0:T(4,128)S(1)} %copy-done.7), custom_call_target="tpu_custom_call" | custom-call | flops 1000000 | bytes 1000000 | tf_op jit(solution)/shard_map/pallas_call | solution.py:188
  (18 shorter events, 0.0 us)
Async XLA Ops:
  2.2 4.8 %collective-permute-start = (bf16[14,8,128]{2,1,0:T(8,128)(2,1)}, bf16[14,8,128]{2,1,0:T(8,128)(2,1)S(1)}, u32[]{:S(2)}, u32[]{:S(2)}) collective-permute-start(bf16[14,8,128]{2,1,0:T(8,128)(2,1)} %get-tuple-element.10._.refs_0_.block_ref), channel_id=1, source_target_pairs={{0,16},{16,0},{32,48},{48,32},{64,80},{80,64},{96,112},{112,96},{1... | collective-permute-start | bytes 86024 | tf_op jit(solution)/shard_map/ppermute | solution.py:199
  2.2 9.3 %collective-permute-start.6 = (bf16[14,8,128]{2,1,0:T(8,128)(2,1)}, bf16[14,8,128]{2,1,0:T(8,128)(2,1)S(1)}, u32[]{:S(2)}, u32[]{:S(2)}) collective-permute-start(bf16[14,8,128]{2,1,0:T(8,128)(2,1)} %get-tuple-element.10._.refs_0_.block_ref), channel_id=1, source_target_pairs={{0,12},{1,13},{2,14},{3,15},{4,0},{5,1},{6,2},{7,3},{8,4},{9,5},{1... | collective-permute-start | bytes 86024 | tf_op jit(solution)/shard_map/ppermute | solution.py:199
  5.3 7.1 %collective-permute-start.5 = (bf16[14,8,128]{2,1,0:T(8,128)(2,1)}, bf16[14,8,128]{2,1,0:T(8,128)(2,1)S(1)}, u32[]{:S(2)}, u32[]{:S(2)}) collective-permute-start(bf16[14,8,128]{2,1,0:T(8,128)(2,1)} %get-tuple-element.10._.refs_0_.block_ref), channel_id=1, source_target_pairs={{0,8},{1,9},{2,10},{3,11},{4,12},{5,13},{6,14},{7,15},{8,0},{9,1},... | collective-permute-start | bytes 86024 | tf_op jit(solution)/shard_map/ppermute | solution.py:199
  6.0 6.4 %collective-permute-start.4 = (bf16[14,8,128]{2,1,0:T(8,128)(2,1)}, bf16[14,8,128]{2,1,0:T(8,128)(2,1)S(1)}, u32[]{:S(2)}, u32[]{:S(2)}) collective-permute-start(bf16[14,8,128]{2,1,0:T(8,128)(2,1)} %get-tuple-element.10._.refs_0_.block_ref), channel_id=1, source_target_pairs={{0,4},{1,5},{2,6},{3,7},{4,8},{5,9},{6,10},{7,11},{8,12},{9,13},{1... | collective-permute-start | bytes 86024 | tf_op jit(solution)/shard_map/ppermute | solution.py:199
  6.9 0.8 %copy-start.3 = (bf16[14,8,128]{2,1,0:T(8,128)(2,1)S(1)}, bf16[14,8,128]{2,1,0:T(8,128)(2,1)}, u32[]{:S(2)}) copy-start(bf16[14,8,128]{2,1,0:T(8,128)(2,1)} %get-tuple-element.10._.refs_0_.block_ref) | copy-start | bytes 86020
  7.7 10.1 %slice-start = ((s8[9830400]{0:T(1024)(128)(4,1)}), s8[4194304]{0:T(1024)(128)(4,1)S(1)}, s32[]{:S(2)}) async-start(s8[9830400]{0:T(1024)(128)(4,1)} %bitcast.4), calls=%async_computation.1 | async-start | bytes 8388608
  7.7 10.1 %slice-start.3 = ((s8[9830400]{0:T(1024)(128)(4,1)}), s8[4194304]{0:T(1024)(128)(4,1)S(1)}, s32[]{:S(2)}) async-start(s8[9830400]{0:T(1024)(128)(4,1)} %bitcast.6), calls=%async_computation.4 | async-start | bytes 8388608
  7.7 10.1 %slice-start.1 = ((s8[9830400]{0:T(1024)(128)(4,1)}), s8[4194304]{0:T(1024)(128)(4,1)S(1)}, s32[]{:S(2)}) async-start(s8[9830400]{0:T(1024)(128)(4,1)} %bitcast.4), calls=%async_computation.2 | async-start | bytes 8388608
  7.8 10.1 %slice-start.2 = ((s8[9830400]{0:T(1024)(128)(4,1)}), s8[1441792]{0:T(1024)(128)(4,1)S(1)}, s32[]{:S(2)}) async-start(s8[9830400]{0:T(1024)(128)(4,1)} %bitcast.4), calls=%async_computation.3 | async-start | bytes 2883584
  7.8 10.1 %slice-start.4 = ((s8[9830400]{0:T(1024)(128)(4,1)}), s8[4194304]{0:T(1024)(128)(4,1)S(1)}, s32[]{:S(2)}) async-start(s8[9830400]{0:T(1024)(128)(4,1)} %bitcast.6), calls=%async_computation.5 | async-start | bytes 8388608
  7.8 10.1 %slice-start.5 = ((s8[9830400]{0:T(1024)(128)(4,1)}), s8[1441792]{0:T(1024)(128)(4,1)S(1)}, s32[]{:S(2)}) async-start(s8[9830400]{0:T(1024)(128)(4,1)} %bitcast.6), calls=%async_computation.6 | async-start | bytes 2883584
  7.8 10.1 %copy-start = (bf16[4,48,3840]{2,1,0:T(8,128)(2,1)S(1)}, bf16[4,48,3840]{2,1,0:T(8,128)(2,1)}, u32[]{:S(2)}) copy-start(bf16[4,48,3840]{2,1,0:T(8,128)(2,1)} %le_ref.1) | copy-start | bytes 4423684
  7.8 10.1 %copy-start.1 = (bf16[4,48,3840]{2,1,0:T(8,128)(2,1)S(1)}, bf16[4,48,3840]{2,1,0:T(8,128)(2,1)}, u32[]{:S(2)}) copy-start(bf16[4,48,3840]{2,1,0:T(8,128)(2,1)} %re_ref.3) | copy-start | bytes 4423684
  7.8 10.1 %copy-start.2 = (bf16[10,4,128,128]{3,2,1,0:T(8,128)(2,1)S(1)}, bf16[10,4,128,128]{3,2,1,0:T(8,128)(2,1)}, u32[]{:S(2)}) copy-start(bf16[10,4,128,128]{3,2,1,0:T(8,128)(2,1)} %refs_4_.1) | copy-start | bytes 3932164
  7.8 10.1 %copy-start.5 = (bf16[4,4,48,48]{3,2,1,0:T(8,128)(2,1)S(1)}, bf16[4,4,48,48]{3,2,1,0:T(8,128)(2,1)}, u32[]{:S(2)}) copy-start(bf16[4,4,48,48]{3,2,1,0:T(8,128)(2,1)} %refs_5_.1) | copy-start | bytes 221188
  7.8 10.1 %copy-start.8 = (f32[10,4]{0,1:T(4,128)S(1)}, f32[10,4]{0,1:T(4,128)}, u32[]{:S(2)}) copy-start(f32[10,4]{0,1:T(4,128)} %param.25) | copy-start | bytes 484
  7.8 10.1 %copy-start.9 = (s32[10,4]{0,1:T(4,128)S(1)}, s32[10,4]{0,1:T(4,128)}, u32[]{:S(2)}) copy-start(s32[10,4]{0,1:T(4,128)} %param.26) | copy-start | bytes 484
  7.9 10.1 %copy-start.10 = (f32[4,4]{1,0:T(4,128)S(1)}, f32[4,4]{1,0:T(4,128)}, u32[]{:S(2)}) copy-start(f32[4,4]{1,0:T(4,128)} %refs_8_.1) | copy-start | bytes 196
  7.9 10.1 %copy-start.11 = (s32[4,4]{1,0:T(4,128)S(1)}, s32[4,4]{1,0:T(4,128)}, u32[]{:S(2)}) copy-start(s32[4,4]{1,0:T(4,128)} %refs_9_.1) | copy-start | bytes 196
  7.9 8.7 %collective-permute-start.3 = (bf16[2,14,8,128]{3,2,1,0:T(8,128)(2,1)S(1)}, bf16[2,14,8,128]{3,2,1,0:T(8,128)(2,1)S(1)}, u32[]{:S(2)}, u32[]{:S(2)}) collective-permute-start(bf16[2,14,8,128]{3,2,1,0:T(8,128)(2,1)S(1)} %shard_map.187.refs_0_), channel_id=1, source_target_pairs={{0,96},{16,112},{32,0},{48,16},{64,32},{80,48},{96,64},{112,80},{1... | collective-permute-start | bytes 172040 | tf_op jit(solution)/shard_map/ppermute | solution.py:199
  10.7 7.1 %collective-permute-start.2 = (bf16[2,14,8,128]{3,2,1,0:T(8,128)(2,1)S(1)}, bf16[2,14,8,128]{3,2,1,0:T(8,128)(2,1)S(1)}, u32[]{:S(2)}, u32[]{:S(2)}) collective-permute-start(bf16[2,14,8,128]{3,2,1,0:T(8,128)(2,1)S(1)} %shard_map.187.refs_0_), channel_id=1, source_target_pairs={{0,64},{16,80},{32,96},{48,112},{64,0},{80,16},{96,32},{112,48},{1... | collective-permute-start | bytes 172040 | tf_op jit(solution)/shard_map/ppermute | solution.py:199
  11.5 6.3 %collective-permute-start.1 = (bf16[2,14,8,128]{3,2,1,0:T(8,128)(2,1)S(1)}, bf16[2,14,8,128]{3,2,1,0:T(8,128)(2,1)S(1)}, u32[]{:S(2)}, u32[]{:S(2)}) collective-permute-start(bf16[2,14,8,128]{3,2,1,0:T(8,128)(2,1)S(1)} %shard_map.187.refs_0_), channel_id=1, source_target_pairs={{0,32},{16,48},{32,64},{48,80},{64,96},{80,112},{96,0},{112,16},{1... | collective-permute-start | bytes 172040 | tf_op jit(solution)/shard_map/ppermute | solution.py:199
  12.4 12.1 %collective-permute-start.9 = (bf16[4,10,8,128]{3,2,1,0:T(8,128)(2,1)S(1)}, bf16[4,10,8,128]{3,2,1,0:T(8,128)(2,1)S(1)}, u32[]{:S(2)}, u32[]{:S(2)}) collective-permute-start(bf16[4,10,8,128]{3,2,1,0:T(8,128)(2,1)S(1)} %shard_map.189.refs_0_), channel_id=1, source_target_pairs={{0,3},{1,0},{2,1},{3,2},{4,7},{5,4},{6,5},{7,6},{8,11},{9,8},{10,9... | collective-permute-start | bytes 245768 | tf_op jit(solution)/shard_map/ppermute | solution.py:199
  16.5 8.0 %collective-permute-start.8 = (bf16[4,10,8,128]{3,2,1,0:T(8,128)(2,1)S(1)}, bf16[4,10,8,128]{3,2,1,0:T(8,128)(2,1)S(1)}, u32[]{:S(2)}, u32[]{:S(2)}) collective-permute-start(bf16[4,10,8,128]{3,2,1,0:T(8,128)(2,1)S(1)} %shard_map.189.refs_0_), channel_id=1, source_target_pairs={{0,2},{1,3},{2,0},{3,1},{4,6},{5,7},{6,4},{7,5},{8,10},{9,11},{10,... | collective-permute-start | bytes 245768 | tf_op jit(solution)/shard_map/ppermute | solution.py:199
  16.5 8.0 %collective-permute-start.7 = (bf16[4,10,8,128]{3,2,1,0:T(8,128)(2,1)S(1)}, bf16[4,10,8,128]{3,2,1,0:T(8,128)(2,1)S(1)}, u32[]{:S(2)}, u32[]{:S(2)}) collective-permute-start(bf16[4,10,8,128]{3,2,1,0:T(8,128)(2,1)S(1)} %shard_map.189.refs_0_), channel_id=1, source_target_pairs={{0,1},{1,2},{2,3},{3,0},{4,5},{5,6},{6,7},{7,4},{8,9},{9,10},{10,1... | collective-permute-start | bytes 245768 | tf_op jit(solution)/shard_map/ppermute | solution.py:199
  24.6 16.2 %copy-start.4 = (bf16[14,8,128]{2,1,0:T(8,128)(2,1)S(1)}, bf16[14,8,128]{2,1,0:T(8,128)(2,1)}, u32[]{:S(2)}) copy-start(bf16[14,8,128]{2,1,0:T(8,128)(2,1)} %get-tuple-element.10._.refs_0_.block_ref) | copy-start | bytes 86020
  24.6 16.2 %copy-start.6 = (f32[10,8,128]{2,1,0:T(8,128)S(1)}, f32[10,8,128]{2,1,0:T(8,128)}, u32[]{:S(2)}) copy-start(f32[10,8,128]{2,1,0:T(8,128)} %get-tuple-element.14.scale_a_ref) | copy-start | bytes 122884
  24.6 16.1 %copy-start.7 = (f32[3,4,48]{2,1,0:T(4,128)S(1)}, f32[3,4,48]{2,1,0:T(4,128)}, u32[]{:S(2)}) copy-start(f32[3,4,48]{2,1,0:T(4,128)} %get-tuple-element.15.scale_e_ref) | copy-start | bytes 6916
